TPU v7x, 32 devices: a whole 2x2x4 slice. The times are simulated.
32 devices in a mesh: dp: 4 (over y, x), seq: 8 (over z, core).
Axes of the slice: x: 2, y: 2, z: 4, core: 2. Of those that a mesh axis runs over, the one named last changes fastest.
Arguments:
- inputs: bfloat16 [4, 8192, 512], P('dp', 'seq'), may hold values from -0.0014648438 to 0.0014648438
- grad_out: bfloat16 [4, 8192, 512], P('dp', 'seq'), may hold values from -6 to 6
- conv_filter: bfloat16 [8192], P('seq'), may hold values from -0.0625 to 0.0625
Outputs:
- grad_input: bfloat16 [4, 8192, 512], P('dp', 'seq')
- grad_filter: float32 [8192], P('seq')
All inputs are finite; a program needn't handle non-finite values.
Results may differ from a plain program's by a relative error of at most 0.0095.
Values may be sent and summed in bfloat16 or wider, within the bound.
No kernel may reach another device: no remote copies, remote signals or barrier semaphores. Data moves between devices by JAX's collectives and lax.ppermute only.
A program may use at most 128 MiB of HBM per device.

v0:
```python
import math

import jax
import jax.numpy as jnp
import numpy as np
from jax import lax
from jax.sharding import PartitionSpec as P

precise = lax.Precision.HIGHEST


def shortened(shard):
    return jax.tree.map(lambda a: a.astype(jnp.bfloat16) if a.dtype == jnp.float32 else a, shard)


def phases(left_index, right_index, period, orient):
    product = left_index * right_index % period
    angles = orient * 2.0 * math.pi / period * product.astype(jnp.float32)
    return (jnp.cos(angles), jnp.sin(angles))


def contract(pattern, matrix, values):
    return jnp.einsum(pattern, matrix, values, precision=precise)


def apply_complex(pattern, matrix, pieces):
    real_part, imag_part = pieces
    return (
        contract(pattern, matrix[0], real_part) - contract(pattern, matrix[1], imag_part),
        contract(pattern, matrix[0], imag_part) + contract(pattern, matrix[1], real_part),
    )


def apply_real(pattern, matrix, values):
    return (contract(pattern, matrix[0], values), contract(pattern, matrix[1], values))


def multiply(left_side, right_side):
    return (
        left_side[0] * right_side[0] - left_side[1] * right_side[1],
        left_side[0] * right_side[1] + left_side[1] * right_side[0],
    )


def split_length(length):
    leading = 1
    for factor in range(1, math.isqrt(length) + 1):
        if length % factor == 0:
            leading = factor
    return leading


def local_transform(pieces, orient):
    real_part, imag_part = pieces
    outside, blocks, length, channels = real_part.shape
    leading = split_length(length)
    trailing = length // leading
    lead_index = jnp.arange(leading, dtype=jnp.int32)
    trail_index = jnp.arange(trailing, dtype=jnp.int32)
    shaped = (
        real_part.reshape(outside, blocks, leading, trailing, channels),
        imag_part.reshape(outside, blocks, leading, trailing, channels),
    )
    sectioned = apply_complex(
        "pa,xkabc->xkpbc", phases(lead_index[:, None], lead_index[None, :], leading, orient), shaped
    )
    twiddle = phases(lead_index[:, None], trail_index[None, :], length, orient)
    twiddle = (twiddle[0][None, None, :, :, None], twiddle[1][None, None, :, :, None])
    sectioned = multiply(sectioned, twiddle)
    sectioned = apply_complex(
        "qb,xkpbc->xkqpc",
        phases(trail_index[:, None], trail_index[None, :], trailing, orient),
        sectioned,
    )
    return (
        sectioned[0].reshape(outside, blocks, length, channels),
        sectioned[1].reshape(outside, blocks, length, channels),
    )


def pair_order(shards):
    device = np.arange(shards, dtype=np.int32)
    partner = np.where(device == 0, shards, 2 * shards - device)
    return np.stack([device, partner], axis=1).reshape(-1).astype(np.int32)


def on_device(inputs, grad_out, conv_filter):
    shards = lax.axis_size("seq")
    position = lax.axis_index("seq")
    doubled = 2 * shards
    tokens = inputs.shape[1]
    period = doubled * tokens
    slab_len = tokens // shards
    pair_index = jnp.asarray(pair_order(shards))
    across = phases(pair_index[:, None], jnp.arange(shards, dtype=jnp.int32)[None, :], doubled, -1)
    global_rows = position * slab_len + jnp.arange(slab_len, dtype=jnp.int32)
    rotation = phases(pair_index[:, None], global_rows[None, :], period, -1)
    rotation = (rotation[0][None, :, :, None], rotation[1][None, :, :, None])
    cut_inputs, cut_grads, cut_filter = (
        lax.all_to_all(inputs[:, None], "seq", split_axis=2, concat_axis=1, tiled=True),
        lax.all_to_all(grad_out[:, None], "seq", split_axis=2, concat_axis=1, tiled=True),
        lax.all_to_all(
            conv_filter.reshape(1, 1, tokens, 1), "seq", split_axis=2, concat_axis=1, tiled=True
        ),
    )
    rows_form = "rn,xnjc->xrjc"
    filter_part = multiply(apply_real(rows_form, across, cut_filter.astype(jnp.float32)), rotation)
    input_part = multiply(apply_real(rows_form, across, cut_inputs.astype(jnp.float32)), rotation)
    grad_part = multiply(apply_real(rows_form, across, cut_grads.astype(jnp.float32)), rotation)
    input_real, input_imag, grad_real, grad_imag, filter_real, filter_imag = (
        lax.all_to_all(
            input_part[0].astype(jnp.bfloat16), "seq", split_axis=1, concat_axis=2, tiled=True
        ).astype(jnp.float32),
        lax.all_to_all(
            input_part[1].astype(jnp.bfloat16), "seq", split_axis=1, concat_axis=2, tiled=True
        ).astype(jnp.float32),
        lax.all_to_all(
            grad_part[0].astype(jnp.bfloat16), "seq", split_axis=1, concat_axis=2, tiled=True
        ).astype(jnp.float32),
        lax.all_to_all(
            grad_part[1].astype(jnp.bfloat16), "seq", split_axis=1, concat_axis=2, tiled=True
        ).astype(jnp.float32),
        lax.all_to_all(
            filter_part[0].astype(jnp.bfloat16), "seq", split_axis=1, concat_axis=2, tiled=True
        ).astype(jnp.float32),
        lax.all_to_all(
            filter_part[1].astype(jnp.bfloat16), "seq", split_axis=1, concat_axis=2, tiled=True
        ).astype(jnp.float32),
    )
    input_spec = local_transform((input_real, input_imag), -1)
    grad_spec = local_transform((grad_real, grad_imag), -1)
    filter_spec = local_transform((filter_real, filter_imag), -1)
    grad_in_spec = (
        filter_spec[0] * grad_spec[0] + filter_spec[1] * grad_spec[1],
        filter_spec[0] * grad_spec[1] - filter_spec[1] * grad_spec[0],
    )
    filter_grad_spec = (
        jnp.sum(
            grad_spec[0] * input_spec[0] + grad_spec[1] * input_spec[1], axis=(0, 3), keepdims=True
        ),
        jnp.sum(
            grad_spec[1] * input_spec[0] - grad_spec[0] * input_spec[1], axis=(0, 3), keepdims=True
        ),
    )
    back_input = local_transform(grad_in_spec, 1)
    back_filter = local_transform(filter_grad_spec, 1)
    own_pair = lax.dynamic_slice_in_dim(pair_index, 2 * position, 2)
    counter_turn = phases(
        own_pair[:, None], jnp.arange(tokens, dtype=jnp.int32)[None, :], period, 1
    )
    counter_turn = (counter_turn[0][None, :, :, None], counter_turn[1][None, :, :, None])
    back_input = multiply(back_input, counter_turn)
    back_filter = multiply(back_filter, counter_turn)
    mid_input_real, mid_input_imag, mid_filter_real, mid_filter_imag = (
        lax.all_to_all(shortened(back_input[0]), "seq", split_axis=2, concat_axis=1, tiled=True),
        lax.all_to_all(shortened(back_input[1]), "seq", split_axis=2, concat_axis=1, tiled=True),
        lax.all_to_all(shortened(back_filter[0]), "seq", split_axis=2, concat_axis=1, tiled=True),
        lax.all_to_all(shortened(back_filter[1]), "seq", split_axis=2, concat_axis=1, tiled=True),
    )
    gather_rows = phases(
        jnp.arange(shards, dtype=jnp.int32)[:, None], pair_index[None, :], doubled, 1
    )
    rows_back = "nr,xrjc->xnjc"
    inverse_scale = 1.0 / period
    input_rows = (
        contract(rows_back, gather_rows[0], mid_input_real)
        - contract(rows_back, gather_rows[1], mid_input_imag)
    ) * inverse_scale
    filter_rows = (
        contract(rows_back, gather_rows[0], mid_filter_real)
        - contract(rows_back, gather_rows[1], mid_filter_imag)
    ) * inverse_scale
    final_input, final_filter = (
        lax.all_to_all(
            shortened(input_rows), "seq", split_axis=1, concat_axis=2, tiled=True
        ).astype(input_rows.dtype),
        lax.all_to_all(
            shortened(filter_rows), "seq", split_axis=1, concat_axis=2, tiled=True
        ).astype(filter_rows.dtype),
    )
    grad_input = final_input[:, 0].astype(jnp.bfloat16)
    grad_filter = final_filter.reshape(tokens)
    grad_filter = lax.psum(grad_filter, "dp")
    return (grad_input, grad_filter)


def solution(mesh):
    placed = (P("dp", "seq", None), P("dp", "seq", None), P("seq"))
    return jax.shard_map(
        on_device,
        mesh=mesh,
        in_specs=placed,
        out_specs=(P("dp", "seq", None), P("seq")),
        check_vma=False,
    )
```

profile of v0, /device:TPU:0, one launch (start us, length us, event | category | flops | bytes accessed | tf_op | source)
XLA Modules:
  0.0 673.5 jit_solution(5725053959151127251)
XLA Ops:
  0.6 4.3 reshape.844
  4.9 6.4 all-to-all-start
  14.7 7.0 %reduce.4 = bf16[1024,512]{1,0:T(8,128)(2,1)S(1)} reduce(bf16[1024,1,1,512]{3,2,1,0:T(2,128)(2,1)S(1)} %bitcast.566, bf16[]{:T(256)} %broadcast.911), dimensions={1,2}, to_apply=%bitcast.547.reduce_sub_computation | reduce | bytes 2097154
  26.7 3.7 all-to-all-start.3
  33.3 8.0 %reduce.3 = bf16[1024,512]{1,0:T(8,128)(2,1)} reduce(bf16[1024,1,1,512]{3,2,1,0:T(2,128)(2,1)S(1)} %bitcast.569, bf16[]{:T(256)} %broadcast.911), dimensions={1,2}, to_apply=%bitcast.546.reduce_sub_computation | reduce | bytes 2097154
  43.9 13.0 %all-to-all-done.3 = bf16[8,2,32768]{2,1,0:T(2,128)(2,1)S(1)} async-done(((bf16[8,2,32768]{2,1,0:T(2,128)(2,1)}), bf16[8,2,32768]{2,1,0:T(2,128)(2,1)S(1)}, u32[]{:S(2)}, u32[]{:S(2)}) %all-to-all-start.3) | async-done | bytes 1048608 | tf_op jit(solution)/shard_map/all_to_all | solution.py:101
  57.9 3.8 all-to-all-start.9
  67.0 4.3 reshape.847
  71.6 3.6 fusion.113
  75.2 3.7 fusion.115
  78.8 9.3 %all-to-all-done.9 = bf16[8,2,32768]{2,1,0:T(2,128)(2,1)S(1)} async-done(((bf16[8,2,32768]{2,1,0:T(2,128)(2,1)}), bf16[8,2,32768]{2,1,0:T(2,128)(2,1)S(1)}, u32[]{:S(2)}, u32[]{:S(2)}) %all-to-all-start.9) | async-done | bytes 1048608 | tf_op jit(solution)/shard_map/all_to_all | solution.py:100
  92.5 4.3 reshape.853
  97.1 3.5 fusion.111
  100.6 5.0 all-to-all-start.1
  105.6 8.6 %fusion.9 = (bf16[1,16,128,512]{3,1,2,0:T(8,128)(2,1)}, bf16[1,16,128,512]{3,1,2,0:T(8,128)(2,1)S(1)}, bf16[1,16,128,512]{3,1,2,0:T(8,128)(2,1)S(1)}, bf16[1,16,128,512]{3,1,2,0:T(8,128)(2,1)}) fusion(f32[16,128,512]{2,0,1:T(8,128)} %fusion.111, f32[16,128]{0,1:T(8,128)S(1)} %copy.258, f32[16,128]{0,1:T(8,128)S(1)} %copy.256, f32[16,128,512]{2,0,1:T(8,128)} %fusion.113, ...), kind=kOutput, calls=%fused_computation.19 | convolution fusion | flops 117442304 | bytes 22036544 | tf_op jit(solution)/shard_map/rn,xnjc->xrjc/dot_general | solution.py:23
  116.8 5.1 all-to-all-start.5
  121.8 4.1 copy.259
  125.9 45.0 %all-to-all-done.5 = bf16[1,16,128,512]{3,2,0,1:T(8,128)(2,1)} async-done(((bf16[1,16,128,512]{3,2,0,1:T(8,128)(2,1)}), bf16[1,16,128,512]{3,2,0,1:T(8,128)(2,1)}, u32[]{:S(2)}, u32[]{:S(2)}) %all-to-all-start.5) | async-done | bytes 2097184 | tf_op jit(solution)/shard_map/all_to_all | solution.py:120
  171.0 4.3 all-to-all-start.4
  175.3 4.2 copy.293
  179.5 44.9 %all-to-all-done.4 = bf16[1,16,128,512]{3,2,0,1:T(8,128)(2,1)} async-done(((bf16[1,16,128,512]{3,2,0,1:T(8,128)(2,1)}), bf16[1,16,128,512]{3,2,0,1:T(8,128)(2,1)}, u32[]{:S(2)}, u32[]{:S(2)}) %all-to-all-start.4) | async-done | bytes 2097184 | tf_op jit(solution)/shard_map/all_to_all | solution.py:117
  224.4 4.4 all-to-all-start.10
  231.5 46.2 %all-to-all-done.10 = bf16[1,16,128,512]{3,2,0,1:T(8,128)(2,1)} async-done(((bf16[1,16,128,512]{3,2,0,1:T(8,128)(2,1)}), bf16[1,16,128,512]{3,2,0,1:T(8,128)(2,1)}, u32[]{:S(2)}, u32[]{:S(2)}) %all-to-all-start.10) | async-done | bytes 2097184 | tf_op jit(solution)/shard_map/all_to_all | solution.py:111
  277.8 4.8 all-to-all-start.11
  293.6 4.8 fusion.85
  298.5 4.9 fusion.91
  303.4 5.3 convolution_add_fusion.1
  308.7 22.4 %all-to-all-done.11 = bf16[1,16,128,512]{3,2,0,1:T(8,128)(2,1)} async-done(((bf16[1,16,128,512]{3,2,0,1:T(8,128)(2,1)}), bf16[1,16,128,512]{3,2,0,1:T(8,128)(2,1)}, u32[]{:S(2)}, u32[]{:S(2)}) %all-to-all-start.11) | async-done | bytes 2097184 | tf_op jit(solution)/shard_map/all_to_all | solution.py:114
  335.8 5.2 convolution_subtract_fusion
  341.0 5.2 convolution_add_fusion
  346.2 13.4 %fusion.5 = (f32[2,32,32,512]{3,1,2,0:T(8,128)S(1)}, f32[2,32,32,512]{3,1,2,0:T(8,128)S(1)}, f32[2,32,32,512]{3,1,2,0:T(8,128)}, f32[2,32,32,512]{3,1,2,0:T(8,128)S(1)}) fusion(f32[2,32,512,32]{2,3,1,0:T(8,128)} %convolution_add_fusion, f32[2,32,512,32]{2,3,1,0:T(8,128)} %convolution_subtract_fusion, f32[32,32]{0,1:T(8,128)S(1)} %copy.251, ...), kind=kOutput, calls=%fused_computation.11 | convolution fusion | flops 416299008 | bytes 35659776 | tf_op jit(solution)/shard_map/pa,xkabc->xkpbc/dot_general | solution.py:23
  359.5 9.0 %fusion.51 = f32[2,32,512,32]{2,3,1,0:T(8,128)S(1)} fusion(f32[2,32,32,512]{3,1,2,0:T(8,128)} %get-tuple-element.18), kind=kOutput, calls=%fused_computation.85 | convolution fusion | flops 402667520 | bytes 8388608 | tf_op jit(solution)/shard_map/qb,xkpbc->xkqpc/dot_general | solution.py:23
  368.5 7.0 %fusion.53 = f32[2,32,512,32]{2,3,1,0:T(8,128)S(1)} fusion(f32[2,32,32,512]{3,1,2,0:T(8,128)S(1)} %copy-done.1), kind=kOutput, calls=%fused_computation.87 | convolution fusion | flops 402667520 | bytes 8388608 | tf_op jit(solution)/shard_map/qb,xkpbc->xkqpc/dot_general | solution.py:23
  375.5 7.2 %fusion.37 = f32[2,32,512,32]{2,3,1,0:T(8,128)S(1)} fusion(f32[2,32,32,512]{3,1,2,0:T(8,128)S(1)} %get-tuple-element.9), kind=kOutput, calls=%fused_computation.71 | convolution fusion | flops 402667520 | bytes 8388608 | tf_op jit(solution)/shard_map/qb,xkpbc->xkqpc/dot_general | solution.py:23
  382.7 7.2 %fusion.35 = f32[2,32,512,32]{2,3,1,0:T(8,128)} fusion(f32[2,32,32,512]{3,1,2,0:T(8,128)S(1)} %get-tuple-element.9), kind=kOutput, calls=%fused_computation.69 | convolution fusion | flops 402667520 | bytes 8388608 | tf_op jit(solution)/shard_map/qb,xkpbc->xkqpc/dot_general | solution.py:23
  389.9 7.4 %fusion.62 = f32[2,32,512,32]{2,3,1,0:T(8,128)S(1)} fusion(f32[2,32,512,32]{2,3,1,0:T(8,128)S(1)} %fusion.51, f32[2,32,32,512]{3,1,2,0:T(8,128)S(1)} %get-tuple-element.19), kind=kOutput, calls=%fused_computation.94 | convolution fusion | flops 403716096 | bytes 12582912 | tf_op jit(solution)/shard_map/qb,xkpbc->xkqpc/dot_general | solution.py:23
  397.3 7.8 %fusion.59 = f32[2,32,512,32]{2,3,1,0:T(8,128)S(1)} fusion(f32[2,32,512,32]{2,3,1,0:T(8,128)S(1)} %fusion.53, f32[2,32,32,512]{3,1,2,0:T(8,128)S(1)} %get-tuple-element.19), kind=kOutput, calls=%fused_computation.93 | convolution fusion | flops 403716096 | bytes 12582912 | tf_op jit(solution)/shard_map/qb,xkpbc->xkqpc/dot_general | solution.py:23
  405.1 7.4 %fusion.69 = f32[2,32,512,32]{2,3,1,0:T(8,128)S(1)} fusion(f32[2,32,512,32]{2,3,1,0:T(8,128)S(1)} %fusion.37, f32[2,32,32,512]{3,1,2,0:T(8,128)S(1)} %get-tuple-element.8), kind=kOutput, calls=%fused_computation.95 | convolution fusion | flops 403716096 | bytes 12582912 | tf_op jit(solution)/shard_map/qb,xkpbc->xkqpc/dot_general | solution.py:23
  412.5 8.8 %fusion.1 = (f32[2,32,32]{1,2,0:T(8,128)S(1)}, f32[2,32,32]{1,2,0:T(8,128)S(1)}) fusion(f32[2,32,512,32]{2,3,1,0:T(8,128)S(1)} %fusion.69, f32[2,32,512,32]{2,3,1,0:T(8,128)S(1)} %fusion.59, f32[2,32,512,32]{2,3,1,0:T(8,128)S(1)} %fusion.62, f32[2,32,512,32]{2,3,1,0:T(8,128)S(1)} %copy-done.5, f32[2,32,32,512]{3,1,2,0:T(8,128)S(1)} %get-tuple-element.8), kind=kOutput, calls=%fused_computation.3 | convolution fusion | flops 412100608 | bytes 20987904 | tf_op jit(solution)/shard_map/qb,xkpbc->xkqpc/dot_general | solution.py:23
  422.9 4.8 fusion.94
  427.7 4.7 fusion.96
  432.4 5.5 fusion.75
  438.0 7.6 %fusion.17 = (f32[2,32,32,512]{3,1,2,0:T(8,128)}, f32[2,32,32,512]{3,1,2,0:T(8,128)S(1)}) fusion(f32[2,32,512,32]{2,3,1,0:T(8,128)S(1)} %fusion.75, f32[32,32]{0,1:T(8,128)S(1)} %copy.276, f32[32,32]{0,1:T(8,128)S(1)} %copy.275, f32[2,32,512,32]{2,3,1,0:T(8,128)S(1)} %fusion.94, f32[2,32,512,32]{2,3,1,0:T(8,128)S(1)} %fusion.59, ...), kind=kOutput, calls=%fused_computation.35 | convolution fusion | flops 413153280 | bytes 25190400 | tf_op jit(solution)/shard_map/pa,xkabc->xkpbc/dot_general | solution.py:23
  445.6 7.0 %fusion.45 = f32[2,32,512,32]{2,3,1,0:T(8,128)} fusion(f32[2,32,32,512]{3,1,2,0:T(8,128)S(1)} %get-tuple-element.11), kind=kOutput, calls=%fused_computation.79 | convolution fusion | flops 402667520 | bytes 8388608 | tf_op jit(solution)/shard_map/qb,xkpbc->xkqpc/dot_general | solution.py:23
  452.6 7.2 %fusion.43 = f32[2,32,512,32]{2,3,1,0:T(8,128)} fusion(f32[2,32,32,512]{3,1,2,0:T(8,128)S(1)} %get-tuple-element.11), kind=kOutput, calls=%fused_computation.77 | convolution fusion | flops 402667520 | bytes 8388608 | tf_op jit(solution)/shard_map/qb,xkpbc->xkqpc/dot_general | solution.py:23
  468.3 12.8 %subtract_bitcast_fusion = f32[1,2,32,32,512]{4,2,3,1,0:T(8,128)} fusion(f32[2,32,512,32]{2,3,1,0:T(8,128)} %fusion.45, f32[2,32,32,512]{3,1,2,0:T(8,128)} %get-tuple-element.10), kind=kOutput, calls=%fused_computation.68 | convolution fusion | flops 403716096 | bytes 12582912 | tf_op jit(solution)/shard_map/qb,xkpbc->xkqpc/dot_general | solution.py:23
  481.1 7.5 %add_bitcast_fusion = f32[1,2,32,32,512]{4,2,3,1,0:T(8,128)} fusion(f32[2,32,512,32]{2,3,1,0:T(8,128)S(1)} %copy-done.4, f32[2,32,32,512]{3,1,2,0:T(8,128)S(1)} %copy-done), kind=kOutput, calls=%fused_computation.67 | convolution fusion | flops 403716096 | bytes 12582912 | tf_op jit(solution)/shard_map/qb,xkpbc->xkqpc/dot_general | solution.py:23
  492.3 6.7 copy.279
  499.0 4.5 copy.282
  503.5 5.0 all-to-all-start.13
  508.5 5.0 fusion.15
  517.0 5.3 all-to-all-start.6
  522.4 5.1 copy.286
  527.5 43.9 %all-to-all-done.6 = bf16[1,2,1024,512]{3,1,0,2:T(2,128)(2,1)S(1)} async-done(((bf16[1,2,1024,512]{3,1,0,2:T(2,128)(2,1)}), bf16[1,2,1024,512]{3,1,0,2:T(2,128)(2,1)S(1)}, u32[]{:S(2)}, u32[]{:S(2)}) %all-to-all-start.6) | async-done | bytes 2097184 | tf_op jit(solution)/shard_map/all_to_all | solution.py:155
  572.7 3.6 all-to-all-start.7
  581.1 3.5 copy.285
  584.6 4.1 reshape.818
  588.8 4.1 fusion.203
  592.8 32.4 %all-to-all-done.7 = bf16[1,2,1024,512]{3,1,0,2:T(2,128)(2,1)S(1)} async-done(((bf16[1,2,1024,512]{3,1,0,2:T(2,128)(2,1)}), bf16[1,2,1024,512]{3,1,0,2:T(2,128)(2,1)S(1)}, u32[]{:S(2)}, u32[]{:S(2)}) %all-to-all-start.7) | async-done | bytes 2097184 | tf_op jit(solution)/shard_map/all_to_all | solution.py:156
  628.9 3.5 copy.288
  632.4 4.1 reshape.819
  640.7 5.0 all-to-all-start.8
  645.7 10.5 %psum.7 = f32[1024]{0:T(1024)} all-reduce(f32[1024]{0:T(1024)S(1)} %bitcast.587), channel_id=1, replica_groups=mesh['dp'=4,'seq'=8] {'dp'}, use_global_device_ids=true, to_apply=%region_2.3 | all-reduce | flops 1024 | bytes 8192 | tf_op jit(solution)/shard_map/psum | solution.py:183
  656.2 16.1 %all-to-all-done.8 = bf16[1,8,128,512]{3,2,0,1:T(8,128)(2,1)S(1)} async-done(((bf16[1,8,128,512]{3,2,0,1:T(8,128)(2,1)}), bf16[1,8,128,512]{3,2,0,1:T(8,128)(2,1)S(1)}, u32[]{:S(2)}, u32[]{:S(2)}) %all-to-all-start.8) | async-done | bytes 1048608 | tf_op jit(solution)/shard_map/all_to_all | solution.py:174
  (124 shorter events, 77.7 us)
Async XLA Ops:
  4.9 21.8 %all-to-all-start = ((bf16[1,1,1024,1]{3,1,0,2:T(2,128)(2,1)}), bf16[1,1,1024,1]{3,1,0,2:T(2,128)(2,1)}, u32[]{:S(2)}, u32[]{:S(2)}) async-start(bf16[1,1,1024,1]{3,1,0,2:T(2,128)(2,1)} %reshape.844), calls=%async_computation | async-start | bytes 1048576 | tf_op jit(solution)/shard_map/all_to_all | solution.py:102
  26.7 30.2 %all-to-all-start.3 = ((bf16[8,2,32768]{2,1,0:T(2,128)(2,1)}), bf16[8,2,32768]{2,1,0:T(2,128)(2,1)S(1)}, u32[]{:S(2)}, u32[]{:S(2)}) async-start(bf16[8,2,32768]{2,1,0:T(2,128)(2,1)} %reshape.846), calls=%async_computation.3 | async-start | bytes 2097152 | tf_op jit(solution)/shard_map/all_to_all | solution.py:101
  33.3 28.4 %copy-start.12 = (s32[16]{0:T(128)S(1)}, s32[16]{0:T(128)}, u32[]{:S(2)}) copy-start(s32[16]{0:T(128)} %constant.141.clone) | copy-start | bytes 196
  56.9 1.0 copy-start.11
  57.9 30.3 %all-to-all-start.9 = ((bf16[8,2,32768]{2,1,0:T(2,128)(2,1)}), bf16[8,2,32768]{2,1,0:T(2,128)(2,1)S(1)}, u32[]{:S(2)}, u32[]{:S(2)}) async-start(bf16[8,2,32768]{2,1,0:T(2,128)(2,1)} %reshape.852), calls=%async_computation.9 | async-start | bytes 2097152 | tf_op jit(solution)/shard_map/all_to_all | solution.py:100
  88.2 1.0 copy-start.10
  89.1 11.5 %all-to-all-start.2 = ((bf16[8,2,128]{2,1,0:T(2,128)(2,1)}), bf16[8,2,128]{2,1,0:T(2,128)(2,1)S(1)}, u32[]{:S(2)}, u32[]{:S(2)}) async-start(bf16[8,2,128]{2,1,0:T(2,128)(2,1)} %bitcast.550), calls=%async_computation.2 | async-start | bytes 8192 | tf_op jit(solution)/shard_map/all_to_all | solution.py:126
  100.6 16.1 %all-to-all-start.1 = ((bf16[8,2,128]{2,1,0:T(2,128)(2,1)}), bf16[8,2,128]{2,1,0:T(2,128)(2,1)S(1)}, u32[]{:S(2)}, u32[]{:S(2)}) async-start(bf16[8,2,128]{2,1,0:T(2,128)(2,1)} %bitcast.551), calls=%async_computation.1 | async-start | bytes 8192 | tf_op jit(solution)/shard_map/all_to_all | solution.py:123
  116.8 54.2 %all-to-all-start.5 = ((bf16[1,16,128,512]{3,2,0,1:T(8,128)(2,1)}), bf16[1,16,128,512]{3,2,0,1:T(8,128)(2,1)}, u32[]{:S(2)}, u32[]{:S(2)}) async-start(bf16[1,16,128,512]{3,2,0,1:T(8,128)(2,1)} %copy.262), calls=%async_computation.5 | async-start | bytes 4194304 | tf_op jit(solution)/shard_map/all_to_all | solution.py:120
  171.0 53.4 %all-to-all-start.4 = ((bf16[1,16,128,512]{3,2,0,1:T(8,128)(2,1)}), bf16[1,16,128,512]{3,2,0,1:T(8,128)(2,1)}, u32[]{:S(2)}, u32[]{:S(2)}) async-start(bf16[1,16,128,512]{3,2,0,1:T(8,128)(2,1)} %copy.259), calls=%async_computation.4 | async-start | bytes 4194304 | tf_op jit(solution)/shard_map/all_to_all | solution.py:117
  224.4 53.4 %all-to-all-start.10 = ((bf16[1,16,128,512]{3,2,0,1:T(8,128)(2,1)}), bf16[1,16,128,512]{3,2,0,1:T(8,128)(2,1)}, u32[]{:S(2)}, u32[]{:S(2)}) async-start(bf16[1,16,128,512]{3,2,0,1:T(8,128)(2,1)} %copy.293), calls=%async_computation.10 | async-start | bytes 4194304 | tf_op jit(solution)/shard_map/all_to_all | solution.py:111
  277.8 53.4 %all-to-all-start.11 = ((bf16[1,16,128,512]{3,2,0,1:T(8,128)(2,1)}), bf16[1,16,128,512]{3,2,0,1:T(8,128)(2,1)}, u32[]{:S(2)}, u32[]{:S(2)}) async-start(bf16[1,16,128,512]{3,2,0,1:T(8,128)(2,1)} %copy.296), calls=%async_computation.11 | async-start | bytes 4194304 | tf_op jit(solution)/shard_map/all_to_all | solution.py:114
  290.8 7.7 %copy-start.2 = (bf16[1,2,8,128,512]{4,3,2,1,0:T(8,128)(2,1)}, bf16[1,2,8,128,512]{4,3,2,1,0:T(8,128)(2,1)S(1)}, u32[]{:S(2)}) copy-start(bf16[1,2,8,128,512]{4,3,2,1,0:T(8,128)(2,1)S(1)} %copy.294) | copy-start | bytes 6291460
  332.9 2.9 copy-start.7
  335.8 5.2 copy-start.3
  359.5 9.0 %copy-start.1 = (f32[2,32,32,512]{3,1,2,0:T(8,128)S(1)}, f32[2,32,32,512]{3,1,2,0:T(8,128)}, u32[]{:S(2)}) copy-start(f32[2,32,32,512]{3,1,2,0:T(8,128)} %get-tuple-element.18) | copy-start | bytes 12582916
  405.1 7.5 %copy-start.5 = (f32[2,32,512,32]{2,3,1,0:T(8,128)S(1)}, f32[2,32,512,32]{2,3,1,0:T(8,128)}, u32[]{:S(2)}) copy-start(f32[2,32,512,32]{2,3,1,0:T(8,128)} %fusion.35) | copy-start | bytes 12582916
  464.9 38.6 %all-to-all-start.12 = ((bf16[8,2,128]{2,1,0:T(2,128)(2,1)}), bf16[8,2,128]{2,1,0:T(2,128)(2,1)S(1)}, u32[]{:S(2)}, u32[]{:S(2)}) async-start(bf16[8,2,128]{2,1,0:T(2,128)(2,1)} %reshape.854), calls=%async_computation.12 | async-start | bytes 8192 | tf_op jit(solution)/shard_map/all_to_all | solution.py:157
  468.2 12.8 %copy-start = (f32[2,32,32,512]{3,1,2,0:T(8,128)S(1)}, f32[2,32,32,512]{3,1,2,0:T(8,128)}, u32[]{:S(2)}) copy-start(f32[2,32,32,512]{3,1,2,0:T(8,128)} %get-tuple-element.10) | copy-start | bytes 12582916
  468.2 12.8 %copy-start.4 = (f32[2,32,512,32]{2,3,1,0:T(8,128)S(1)}, f32[2,32,512,32]{2,3,1,0:T(8,128)}, u32[]{:S(2)}) copy-start(f32[2,32,512,32]{2,3,1,0:T(8,128)} %fusion.43) | copy-start | bytes 12582916
  492.3 6.7 copy-start.6
  503.5 13.5 %all-to-all-start.13 = ((bf16[8,2,128]{2,1,0:T(2,128)(2,1)}), bf16[8,2,128]{2,1,0:T(2,128)(2,1)S(1)}, u32[]{:S(2)}, u32[]{:S(2)}) async-start(bf16[8,2,128]{2,1,0:T(2,128)(2,1)} %reshape.856), calls=%async_computation.13 | async-start | bytes 8192 | tf_op jit(solution)/shard_map/all_to_all | solution.py:158
  517.0 54.3 %all-to-all-start.6 = ((bf16[1,2,1024,512]{3,1,0,2:T(2,128)(2,1)}), bf16[1,2,1024,512]{3,1,0,2:T(2,128)(2,1)S(1)}, u32[]{:S(2)}, u32[]{:S(2)}) async-start(bf16[1,2,1024,512]{3,1,0,2:T(2,128)(2,1)} %copy.283), calls=%async_computation.6 | async-start | bytes 4194304 | tf_op jit(solution)/shard_map/all_to_all | solution.py:155
  571.4 1.3 copy-start.8
  572.7 52.6 %all-to-all-start.7 = ((bf16[1,2,1024,512]{3,1,0,2:T(2,128)(2,1)}), bf16[1,2,1024,512]{3,1,0,2:T(2,128)(2,1)S(1)}, u32[]{:S(2)}, u32[]{:S(2)}) async-start(bf16[1,2,1024,512]{3,1,0,2:T(2,128)(2,1)} %copy.286), calls=%async_computation.7 | async-start | bytes 4194304 | tf_op jit(solution)/shard_map/all_to_all | solution.py:156
  625.2 15.5 %all-to-all-start.14 = ((bf16[1,8,128,1]{2,3,0,1:T(2,128)(2,1)}), bf16[1,8,128,1]{2,3,0,1:T(2,128)(2,1)S(1)}, u32[]{:S(2)}, u32[]{:S(2)}) async-start(bf16[1,8,128,1]{2,3,0,1:T(2,128)(2,1)} %copy.319), calls=%async_computation.14 | async-start | bytes 8192 | tf_op jit(solution)/shard_map/all_to_all | solution.py:177
  628.9 7.7 %copy-start.9 = (f32[128,512,8]{1,2,0:T(8,128)S(1)}, f32[128,512,8]{1,2,0:T(8,128)}, u32[]{:S(2)}) copy-start(f32[128,512,8]{1,2,0:T(8,128)} %fusion.203) | copy-start | bytes 6291460
  640.7 31.6 %all-to-all-start.8 = ((bf16[1,8,128,512]{3,2,0,1:T(8,128)(2,1)}), bf16[1,8,128,512]{3,2,0,1:T(8,128)(2,1)S(1)}, u32[]{:S(2)}, u32[]{:S(2)}) async-start(bf16[1,8,128,512]{3,2,0,1:T(8,128)(2,1)} %copy.289), calls=%async_computation.8 | async-start | bytes 2097152 | tf_op jit(solution)/shard_map/all_to_all | solution.py:174
where the time goes:
time: 683 us; the launch traced here: 674 us
  waiting for transfers between devices  277 us (41%)
  matrix products  195 us (29%)
  local copies, waits for them, and re-layouts  95.1 us (14%)
  starting transfers between devices  66.4 us (10%)
  other arithmetic  28.6 us (4%)
  blocking collectives  10.5 us (2%)
    dot_general x50, matrix products, contract(): return jnp.einsum(pattern, matrix, values, precision=precise)  195 us
    all_to_all x1, waiting for transfers between devices, on_device(): lax.all_to_all(input_part[0].astype(jnp.bfloat16), 'seq', split_axis=1, c...  46.2 us
    all_to_all x1, waiting for transfers between devices, on_device(): lax.all_to_all(grad_part[1].astype(jnp.bfloat16), 'seq', split_axis=1, co...  45 us
    all_to_all x1, waiting for transfers between devices, on_device(): lax.all_to_all(grad_part[0].astype(jnp.bfloat16), 'seq', split_axis=1, co...  44.9 us
    all_to_all x1, waiting for transfers between devices, on_device(): lax.all_to_all(shortened(back_input[0]), 'seq', split_axis=2, concat_axis...  43.9 us
    all_to_all x1, waiting for transfers between devices, on_device(): lax.all_to_all(shortened(back_input[1]), 'seq', split_axis=2, concat_axis...  32.4 us
    unnamed x46, local copies, waits for them, and re-layouts  22.5 us
    all_to_all x1, waiting for transfers between devices, on_device(): lax.all_to_all(input_part[1].astype(jnp.bfloat16), 'seq', split_axis=1, c...  22.4 us
  transfers between devices with their start and end apart: 15, of which 10 were waited for; matrix products, arithmetic and copies ran while one was open for 26% of the time, Pallas kernels for 0%

commit v1 on v0

v1 whole, which is shorter than its diff:
```python
import jax
import jax.numpy as jnp
from jax import lax
from jax.experimental import pallas as pl
from jax.experimental.pallas import tpu as pltpu
from jax.sharding import PartitionSpec as P

TILE = 256


def low_bit(value):
    return value & -value


def reach(chip, core, chips):
    span = low_bit(chip + 1) if core == 0 else low_bit(chip)
    return span if span < chips else 0


def place(chips):
    index = lax.axis_index("seq")
    chip, core = index // 2, index % 2
    span = jnp.where(core == 0, low_bit(chip + 1), low_bit(chip))
    return core, jnp.where(span < chips, span, 0)


def hops(chips, distance, kind):
    pairs = []
    for chip in range(chips):
        for core in range(2):
            span = reach(chip, core, chips)
            own_first = span - 1
            limit = {"grad": (span, own_first), "rest": (own_first, span)}[kind][core]
            if distance <= limit:
                pairs.append((chip, core))
    return pairs


def levels_of(most):
    level = 1
    while level <= most:
        yield level
        level *= 2


def dot(left, right):
    return jnp.dot(left, right, preferred_element_type=jnp.float32)


def dot_nt(left, right):
    return lax.dot_general(left, right, (((1,), (1,)), ((), ())), preferred_element_type=jnp.float32)


def local_kernel(filter_ref, grad_ref, input_ref, stair_ref, out_ref, lag_ref, skew_ref):
    slab = grad_ref.shape[0]
    length = stair_ref.shape[1]
    width = skew_ref.shape[1]
    row = jnp.broadcast_to(filter_ref[...], (8, width))
    skew_ref[...] = pltpu.roll(row, 0, 1, stride=1, stride_axis=0)

    def rows(step, carry):
        low = skew_ref[...]
        high = pltpu.roll(low, 8, 1)
        both = jnp.concatenate([low[:, :length], high[:, :length]], axis=0)
        stair_ref[pl.ds(pl.multiple_of(step * 16, 16), 16), :] = both.astype(stair_ref.dtype)
        skew_ref[...] = pltpu.roll(high, 8, 1)
        return carry

    lax.fori_loop(0, TILE // 16, rows, 0)
    lag_ref[...] = jnp.zeros_like(lag_ref)
    for start in range(0, slab, TILE):
        rest = grad_ref[start:, :]
        out_ref[start : start + TILE, :] = dot(stair_ref[:, : slab - start], rest)
        lag_ref[:, : slab - start] += dot_nt(input_ref[start : start + TILE, :], rest)


def sources(core, own, received):
    return list(received) if core == 0 else [own, *received[:-1]]


def cross_kernel(chips, stair_ref, grad_ref, *refs):
    most = chips // 2
    received, sent, kept_ref = refs[:most], refs[most : 2 * most], refs[2 * most]
    slab = grad_ref.shape[0]
    blocks = slab // TILE
    core, span = place(chips)

    @pl.when((core == 1) | (span == 0))
    def _():
        kept_ref[...] = jnp.zeros_like(kept_ref)

    for side in range(2):
        grads = sources(side, grad_ref, received)
        targets = [kept_ref, *sent[:-1]] if side == 0 else list(sent)
        for level in levels_of(most):

            @pl.when((core == side) & (span == level))
            def _(grads=grads, targets=targets, level=level):
                for low in range(level):

                    def block(step, carry, low=low):
                        lag = low * blocks + blocks - step
                        total = 0.0
                        for high in range(level):
                            at = pl.multiple_of((lag + high * blocks) * TILE, TILE)
                            total += dot(stair_ref[:, pl.ds(at, slab)], grads[high][...])
                        rows = pl.ds(pl.multiple_of(step * TILE, TILE), TILE)
                        targets[low][rows, :] = total.astype(targets[low].dtype)
                        return carry

                    lax.fori_loop(0, blocks, block, 0)


def lag_kernel(chips, local_ref, grad_ref, input_ref, *refs):
    most = chips // 2
    got_grads, got_inputs = refs[:most], refs[most : 2 * most]
    out_ref, lag_ref, skew_ref = refs[2 * most :]
    slab = grad_ref.shape[0]
    blocks = slab // TILE
    length = lag_ref.shape[1]
    core, span = place(chips)
    lag_ref[:, :slab] = local_ref[...]
    lag_ref[:, slab:] = jnp.zeros((TILE, length - slab), jnp.float32)
    for side in range(2):
        grads = sources(side, grad_ref, got_grads)
        inputs = sources(1 - side, input_ref, got_inputs)
        for level in levels_of(most):

            @pl.when((core == side) & (span == level))
            def _(grads=grads, inputs=inputs, level=level):
                for low in range(level):

                    def block(step, carry, low=low):
                        lag = low * blocks + blocks - step
                        rows = pl.ds(pl.multiple_of(step * TILE, TILE), TILE)
                        left = inputs[low][rows, :]
                        for high in range(level):
                            at = pl.multiple_of((lag + high * blocks) * TILE, TILE)
                            lag_ref[:, pl.ds(at, slab)] += dot_nt(left, grads[high][...])
                        return carry

                    lax.fori_loop(0, blocks, block, 0)

    width = skew_ref.shape[1]
    skew_ref[...] = jnp.zeros_like(skew_ref)

    def rows(step, carry):
        group = TILE // 8 - 1 - step
        moved = pltpu.roll(skew_ref[...], width - 8, 1)
        part = lag_ref[pl.ds(pl.multiple_of(group * 8, 8), 8), :]
        skew_ref[...] = moved + jnp.concatenate([part, jnp.zeros((8, width - length), jnp.float32)], axis=1)
        return carry

    lax.fori_loop(0, TILE // 8, rows, 0)
    total = skew_ref[0:1, :]
    for row in range(1, 8):
        total += pltpu.roll(skew_ref[row : row + 1, :], width - row, 1)
    out_ref[...] = total[:, :length]


def finish_kernel(local_ref, kept_ref, *refs):
    total = local_ref[...] + kept_ref[...].astype(jnp.float32)
    for ref in refs[:-1]:
        total += ref[...].astype(jnp.float32)
    refs[-1][...] = total.astype(refs[-1].dtype)


def call(kernel, outs, scratch=()):
    return pl.pallas_call(kernel, out_shape=outs, scratch_shapes=scratch)


def on_device(inputs, grad_out, conv_filter):
    shards = lax.axis_size("seq")
    chips = shards // 2
    most = chips // 2
    core = lax.axis_index("seq") % 2
    tokens, channels = inputs.shape[1], inputs.shape[2]
    half = channels // 2
    slab = 2 * tokens
    length = shards * tokens
    swap = [(index, index ^ 1) for index in range(shards)]

    def to_slab(array):
        mine = lax.dynamic_slice_in_dim(array[0], core * half, half, 1)
        other = lax.dynamic_slice_in_dim(array[0], (1 - core) * half, half, 1)
        other = lax.ppermute(other, "seq", swap)
        return jnp.where(
            core == 0, jnp.concatenate([mine, other], 0), jnp.concatenate([other, mine], 0)
        )

    def shift(array, distance, kind, sign):
        pairs = []
        for chip, side in hops(chips, distance, kind):
            away = 2 * (chip + distance * (1 if kind == "grad" else -1)) + side
            here = 2 * chip + side
            pairs.append((away, here) if sign > 0 else (here, away))
        return lax.ppermute(array, "seq", pairs) if pairs else jnp.zeros_like(array)

    whole_filter = lax.all_gather(conv_filter, "seq", tiled=True)
    grads = to_slab(grad_out)
    values = to_slab(inputs)
    got_grads = [shift(grads, distance, "grad", 1) for distance in range(1, most + 1)]
    got_values = [shift(values, distance, "rest", 1) for distance in range(1, most + 1)]
    row = jnp.pad(whole_filter.astype(jnp.float32).reshape(1, length), ((0, 0), (0, TILE)))
    stair, local_out, local_lag = call(
        local_kernel,
        (
            jax.ShapeDtypeStruct((TILE, length), jnp.bfloat16),
            jax.ShapeDtypeStruct((slab, half), jnp.float32),
            jax.ShapeDtypeStruct((TILE, slab), jnp.float32),
        ),
        (pltpu.VMEM((8, length + TILE), jnp.float32),),
    )(row, grads, values)
    piece = jax.ShapeDtypeStruct((slab, half), jnp.bfloat16)
    *sent, kept = call(
        lambda *refs: cross_kernel(chips, *refs),
        (*([piece] * most), jax.ShapeDtypeStruct((slab, half), jnp.float32)),
    )(stair, grads, *got_grads)
    parts = [shift(array, index + 1, "rest", -1) for index, array in enumerate(sent)]
    filter_part = call(
        lambda *refs: lag_kernel(chips, *refs),
        jax.ShapeDtypeStruct((1, length), jnp.float32),
        (pltpu.VMEM((TILE, length), jnp.float32), pltpu.VMEM((8, length + TILE), jnp.float32)),
    )(local_lag, grads, values, *got_grads, *got_values)
    spread = lax.all_to_all(filter_part.reshape(shards, tokens), "seq", 0, 0, tiled=True)
    grad_filter = jnp.sum(lax.all_gather(jnp.sum(spread, axis=0), "dp"), axis=0)
    result = call(finish_kernel, piece)(local_out, kept, *parts)
    mine = lax.dynamic_slice_in_dim(result, core * tokens, tokens, 0)
    other = lax.dynamic_slice_in_dim(result, (1 - core) * tokens, tokens, 0)
    other = lax.ppermute(other, "seq", swap)
    grad_input = jnp.where(
        core == 0, jnp.concatenate([mine, other], 1), jnp.concatenate([other, mine], 1)
    )
    return grad_input[None], grad_filter


def solution(mesh):
    placed = (P("dp", "seq", None), P("dp", "seq", None), P("seq"))
    return jax.shard_map(
        on_device,
        mesh=mesh,
        in_specs=placed,
        out_specs=(P("dp", "seq", None), P("seq")),
        check_vma=False,
    )
```

time: 683 us -> 148 us (0.22); the launches traced: 674 us -> 148 us
  waiting for transfers between devices: 277 us -> 19.7 us
  matrix products: 195 us -> 0 us
  local copies, waits for them, and re-layouts: 95.1 us -> 6.5 us
  Pallas kernels: 0 us -> 37.2 us
  blocking collectives: 10.5 us -> 38.3 us
  starting transfers between devices: 66.4 us -> 39.9 us
  other arithmetic: 28.6 us -> 5.24 us
    all_to_all x15 -> x0, waiting for transfers between devices: 277 us -> none  [the longest x1 46.2 us: on_device(): lax.all_to_all(input_part[0].astype(jnp.bfloat16), 'seq', split_axis=1, c...]
    dot_general x50 -> x0, matrix products: 195 us -> none  [contract(): return jnp.einsum(pattern, matrix, values, precision=precise)]
    all_to_all x15 -> x0, starting transfers between devices: 66.4 us -> none  [the longest x1 6.35 us: on_device(): lax.all_to_all(conv_filter.reshape(1, 1, tokens, 1), 'seq', split_axis=2,...]
    ppermute x0 -> x9, starting transfers between devices: none -> 39.9 us  [the longest x6 39.2 us: shift(): return lax.ppermute(array, 'seq', pairs) if pairs else jnp.zeros_like(array)]
    pallas_call x0 -> x4, Pallas kernels: none -> 37.2 us  [the longest x1 13.6 us: on_device(): call(lambda *refs: lag_kernel(chips, *refs), jax.ShapeDtypeStruct((1, len...]
    convert_element_type x12 -> x0, local copies, waits for them, and re-layouts: 25.2 us -> none  [the longest x6 11.9 us: shortened(): a.astype(jnp.bfloat16)]
    all_gather x0 -> x2, blocking collectives: none -> 22.7 us  [the longest x1 14.5 us: on_device(): whole_filter = lax.all_gather(conv_filter, 'seq', tiled=True)]
    unnamed x46 -> x18, local copies, waits for them, and re-layouts: 22.5 us -> 2.78 us
  transfers between devices with their start and end apart: 15 -> 9, of which waited for: 10 -> 2; matrix products, arithmetic and copies ran while one was open for 26% -> 4% of each run, Pallas kernels for 0% -> 19%
where the time goes in v1:
time: 148 us
  starting transfers between devices  39.9 us (27%)
  blocking collectives  38.3 us (26%)
  Pallas kernels  37.2 us (25%)
  waiting for transfers between devices  19.7 us (13%)
  local copies, waits for them, and re-layouts  6.5 us (4%)
  other arithmetic  5.24 us (4%)
    ppermute x6, starting transfers between devices, shift(): return lax.ppermute(array, 'seq', pairs) if pairs else jnp.zeros_like(array)  39.2 us
    ppermute x6, waiting for transfers between devices, shift(): return lax.ppermute(array, 'seq', pairs) if pairs else jnp.zeros_like(array)  19.7 us
    all_to_all x1, blocking collectives, on_device(): lax.all_to_all(filter_part.reshape(shards, tokens), 'seq', 0, 0, tiled=True)  15.6 us
    all_gather x1, blocking collectives, on_device(): whole_filter = lax.all_gather(conv_filter, 'seq', tiled=True)  14.5 us
    pallas_call x1, Pallas kernels, on_device(): call(lambda *refs: lag_kernel(chips, *refs), jax.ShapeDtypeStruct((1, len...  13.6 us
    pallas_call x1, Pallas kernels, on_device(): call(local_kernel, (jax.ShapeDtypeStruct((TILE, length), jnp.bfloat16), j...  10.7 us
    pallas_call x1, Pallas kernels, on_device(): call(lambda *refs: cross_kernel(chips, *refs), (*[piece] * most, jax.Shap...  8.81 us
    all_gather x1, blocking collectives, on_device(): grad_filter = jnp.sum(lax.all_gather(jnp.sum(spread, axis=0), 'dp'), axis=0)  8.2 us
  transfers between devices with their start and end apart: 9, of which 2 were waited for; matrix products, arithmetic and copies ran while one was open for 4% of the time, Pallas kernels for 19%

profile of v1, /device:TPU:0, one launch (start us, length us, event | category | flops | bytes accessed | tf_op | source)
XLA Modules:
  0.0 147.6 jit_solution(6929928013838938758)
XLA Ops:
  0.6 0.0 copy-start.7
  0.7 0.0 copy-start.8
  0.7 1.4 dynamic-slice_bitcast_fusion.4
  2.0 0.6 collective-permute-start
  2.6 0.0 copy-done.7
  2.6 1.1 dynamic-slice_bitcast_fusion.2
  3.7 0.1 collective-permute-start.1
  3.7 0.0 copy-done.8
  3.7 0.0 copy-start.4
  3.7 14.5 %all_gather.9 = bf16[8192]{0:T(1024)(128)(2,1)S(1)} all-gather(bf16[1024]{0:T(1024)(128)(2,1)S(1)} %copy-done.8), channel_id=1, replica_groups=mesh['dp'=4,'seq'=8] {'seq'}, dimensions={0}, use_global_device_ids=true | all-gather | bytes 18432 | tf_op jit(solution)/shard_map/all_gather | solution.py:199
  18.3 0.0 collective-permute-done
  18.3 0.2 maximum_select_fusion.grad_ref.refs_1_
  18.6 0.0 copy-start
  18.6 1.3 collective-permute-start.2
  19.9 0.7 collective-permute-start.3
  20.6 0.6 pad_convert_fusion.filter_ref
  21.2 0.0 collective-permute-done.1
  21.2 0.0 copy-done.4
  21.2 2.5 %maximum_select_fusion.1.input_ref.refs_2_ = bf16[2048,256]{1,0:T(8,128)(2,1)} fusion(bf16[1024,256]{1,0:T(8,128)(2,1)} %collective-permute-done.1, bf16[1024,256]{1,0:T(8,128)(2,1)S(1)} %copy-done.4, pred[]{:T(512)S(6)} %eq.4), kind=kLoop, calls=%fused_computation.1 | loop fusion | flops 4718592 | bytes 2097153 | tf_op jit(solution)/shard_map/jit(_where)/select_n | solution.py:187
  23.8 0.0 copy-done
  23.8 10.7 %shard_map.50 = (bf16[256,8192]{1,0:T(8,128)(2,1)}, f32[2048,256]{1,0:T(8,128)}, f32[256,2048]{1,0:T(8,128)}) custom-call(f32[1,8448]{1,0:T(1,128)} %pad_convert_fusion.filter_ref, bf16[2048,256]{1,0:T(8,128)(2,1)} %copy-done, bf16[2048,256]{1,0:T(8,128)(2,1)} %maximum_select_fusion.1.input_ref.refs_2_), custom_call_target="tpu_custom_call" | custom-call | tf_op jit(solution)/shard_map/pallas_call | solution.py:205
  34.4 0.8 collective-permute-done.2.refs_2_.refs_3_
  35.3 0.0 copy-start.2
  35.3 0.0 collective-permute-done.3.refs_3_.refs_4_
  35.3 0.0 copy-start.3
  35.3 1.0 copy-done.2
  36.3 0.4 copy-done.3
  36.7 0.0 copy-start.1
  36.7 8.8 %shard_map.51 = (bf16[2048,256]{1,0:T(8,128)(2,1)}, bf16[2048,256]{1,0:T(8,128)(2,1)}, f32[2048,256]{1,0:T(8,128)}) custom-call(bf16[256,8192]{1,0:T(8,128)(2,1)} %get-tuple-element.9.refs_0_, bf16[2048,256]{1,0:T(8,128)(2,1)} %copy-done, bf16[2048,256]{1,0:T(8,128)(2,1)} %copy-done.2, bf16[2048,256]{1,0:T(8,128)(2,1)} %copy-done.3), custom_call_target="tpu_custom_call" | custom-call | tf_op jit(solution)/shard_map/pallas_call | solution.py:215
  45.5 1.3 collective-permute-start.4
  46.8 0.7 collective-permute-start.5
  47.5 0.0 copy-done.1
  47.6 33.5 %collective-permute-start.7 = (bf16[2048,256]{1,0:T(8,128)(2,1)S(1)}, bf16[2048,256]{1,0:T(8,128)(2,1)}, u32[]{:S(2)}, u32[]{:S(2)}) collective-permute-start(bf16[2048,256]{1,0:T(8,128)(2,1)S(1)} %copy-done.1), channel_id=1, source_target_pairs={{0,2},{1,3},{3,5},{5,7},{8,10},{9,11},{11,13},{13,15},{16,18},{17,... | collective-permute-start | bytes 3145736 | tf_op jit(solution)/shard_map/ppermute | solution.py:197
  81.0 1.7 %collective-permute-start.8 = (bf16[2048,256]{1,0:T(8,128)(2,1)S(1)}, bf16[2048,256]{1,0:T(8,128)(2,1)}, u32[]{:S(2)}, u32[]{:S(2)}) collective-permute-start(bf16[2048,256]{1,0:T(8,128)(2,1)S(1)} %copy-done.1), channel_id=1, source_target_pairs={{1,5},{9,13},{17,21},{25,29}} | collective-permute-start | bytes 3145736 | tf_op jit(solution)/shard_map/ppermute | solution.py:197
  82.7 18.8 %collective-permute-done.4.refs_0_ = bf16[2048,256]{1,0:T(8,128)(2,1)S(1)} collective-permute-done((bf16[2048,256]{1,0:T(8,128)(2,1)}, bf16[2048,256]{1,0:T(8,128)(2,1)S(1)}, u32[]{:S(2)}, u32[]{:S(2)}) %collective-permute-start.4) | collective-permute-done | bytes 1048608 | tf_op jit(solution)/shard_map/ppermute | solution.py:197
  101.5 0.0 copy-start.5
  101.5 0.0 collective-permute-done.5.refs_1_
  101.5 0.0 copy-start.6
  101.5 1.0 copy-done.5
  102.5 0.4 copy-done.6
  102.8 4.1 %shard_map.52 = bf16[2048,256]{1,0:T(8,128)(2,1)} custom-call(f32[2048,256]{1,0:T(8,128)} %get-tuple-element.8.local_ref, f32[2048,256]{1,0:T(8,128)} %get-tuple-element.10.kept_ref, bf16[2048,256]{1,0:T(8,128)(2,1)} %copy-done.5, bf16[2048,256]{1,0:T(8,128)(2,1)} %copy-done.6), custom_call_target="tpu_custom_call" | custom-call | tf_op jit(solution)/shard_map/pallas_call | solution.py:227
  106.9 1.3 dynamic-slice_bitcast_fusion
  108.2 0.1 collective-permute-start.6
  108.3 0.0 collective-permute-done.7.refs_5_
  108.3 0.0 collective-permute-done.8.refs_6_
  108.3 13.6 %shard_map.53 = f32[1,8192]{1,0:T(1,128)} custom-call(f32[256,2048]{1,0:T(8,128)} %get-tuple-element.13.refs_0_, bf16[2048,256]{1,0:T(8,128)(2,1)} %copy-done, bf16[2048,256]{1,0:T(8,128)(2,1)} %maximum_select_fusion.1.input_ref.refs_2_, bf16[2048,256]{1,0:T(8,128)(2,1)} %copy-done.2, bf16[2048,256]{1,0:T(8,128)(2,1)} %copy-done.3, ...), custom_call_target="tpu_custom_call" | custom-call | tf_op jit(solution)/shard_map/pallas_call | solution.py:220
  121.9 15.6 %all_to_all.9 = f32[8,1,1024]{2,1,0:T(1,128)S(1)} all-to-all(f32[8,1,1024]{2,1,0:T(1,128)} %bitcast.13), channel_id=1, replica_groups=mesh['dp'=4,'seq'=8] {'seq'}, dimensions={0} | all-to-all | bytes 65536 | tf_op jit(solution)/shard_map/all_to_all | solution.py:225
  137.5 8.2 %all-gather = f32[4096]{0:T(1024)S(1)} all-gather(f32[1024]{0:T(1024)S(1)} %reduce_sum.18), channel_id=2, replica_groups=mesh['dp'=4,'seq'=8] {'dp'}, dimensions={0}, use_global_device_ids=true | all-gather | bytes 20480 | tf_op jit(solution)/shard_map/all_gather | solution.py:226
  145.7 0.6 reduce_sum.19
  146.3 0.0 collective-permute-done.6
  146.4 1.2 maximum_select_fusion.2
  (3 shorter events, 0.1 us)
Async XLA Ops:
  0.6 2.0 %copy-start.7 = (bf16[1,1024,512]{2,1,0:T(8,128)(2,1)S(1)}, bf16[1,1024,512]{2,1,0:T(8,128)(2,1)}, u32[]{:S(2)}) copy-start(bf16[1,1024,512]{2,1,0:T(8,128)(2,1)} %param.3) | copy-start | bytes 3145732
  0.7 3.1 %copy-start.8 = (bf16[1024]{0:T(1024)(128)(2,1)S(1)}, bf16[1024]{0:T(1024)(128)(2,1)}, u32[]{:S(2)}) copy-start(bf16[1024]{0:T(1024)(128)(2,1)} %param.5) | copy-start | bytes 6148
  2.0 16.3 %collective-permute-start = (bf16[1024,256]{1,0:T(8,128)(2,1)S(1)}, bf16[1024,256]{1,0:T(8,128)(2,1)S(1)}, u32[]{:S(2)}, u32[]{:S(2)}) collective-permute-start(bf16[1024,256]{1,0:T(8,128)(2,1)S(1)} %get-tuple-element.19), channel_id=1, source_target_pairs={{0,1},{1,0},{2,3},{3,2},{4,5},{5,4},{6,7},{7,6},{8,9},{9,8},{10,11... | collective-permute-start | bytes 1572872 | tf_op jit(solution)/shard_map/ppermute | solution.py:186
  3.7 17.6 %collective-permute-start.1 = (bf16[1024,256]{1,0:T(8,128)(2,1)}, bf16[1024,256]{1,0:T(8,128)(2,1)}, u32[]{:S(2)}, u32[]{:S(2)}) collective-permute-start(bf16[1024,256]{1,0:T(8,128)(2,1)} %get-tuple-element.17), channel_id=1, source_target_pairs={{0,1},{1,0},{2,3},{3,2},{4,5},{5,4},{6,7},{7,6},{8,9},{9,8},{10,11... | collective-permute-start | bytes 1572872 | tf_op jit(solution)/shard_map/ppermute | solution.py:186
  3.7 17.5 %copy-start.4 = (bf16[1024,256]{1,0:T(8,128)(2,1)S(1)}, bf16[1024,256]{1,0:T(8,128)(2,1)}, u32[]{:S(2)}) copy-start(bf16[1024,256]{1,0:T(8,128)(2,1)} %get-tuple-element.16) | copy-start | bytes 1572868
  18.6 5.2 %copy-start = (bf16[2048,256]{1,0:T(8,128)(2,1)}, bf16[2048,256]{1,0:T(8,128)(2,1)S(1)}, u32[]{:S(2)}) copy-start(bf16[2048,256]{1,0:T(8,128)(2,1)S(1)} %maximum_select_fusion.grad_ref.refs_1_) | copy-start | bytes 3145732
  18.6 16.7 %collective-permute-start.2 = (bf16[2048,256]{1,0:T(8,128)(2,1)S(1)}, bf16[2048,256]{1,0:T(8,128)(2,1)S(1)}, u32[]{:S(2)}, u32[]{:S(2)}) collective-permute-start(bf16[2048,256]{1,0:T(8,128)(2,1)S(1)} %maximum_select_fusion.grad_ref.refs_1_), channel_id=1, source_target_pairs={{2,0},{4,2},{6,4},{7,5},{10,8},{12,10},{14,12},{15,13},{18,16},{20... | collective-permute-start | bytes 3145736 | tf_op jit(solution)/shard_map/ppermute | solution.py:197
  19.9 15.4 %collective-permute-start.3 = (bf16[2048,256]{1,0:T(8,128)(2,1)S(1)}, bf16[2048,256]{1,0:T(8,128)(2,1)S(1)}, u32[]{:S(2)}, u32[]{:S(2)}) collective-permute-start(bf16[2048,256]{1,0:T(8,128)(2,1)S(1)} %maximum_select_fusion.grad_ref.refs_1_), channel_id=1, source_target_pairs={{6,2},{14,10},{22,18},{30,26}} | collective-permute-start | bytes 3145736 | tf_op jit(solution)/shard_map/ppermute | solution.py:197
  35.3 1.0 copy-start.2
  35.3 1.4 copy-start.3
  36.7 10.8 %copy-start.1 = (bf16[2048,256]{1,0:T(8,128)(2,1)S(1)}, bf16[2048,256]{1,0:T(8,128)(2,1)}, u32[]{:S(2)}) copy-start(bf16[2048,256]{1,0:T(8,128)(2,1)} %maximum_select_fusion.1.input_ref.refs_2_) | copy-start | bytes 3145732
  45.5 56.0 %collective-permute-start.4 = (bf16[2048,256]{1,0:T(8,128)(2,1)}, bf16[2048,256]{1,0:T(8,128)(2,1)S(1)}, u32[]{:S(2)}, u32[]{:S(2)}) collective-permute-start(bf16[2048,256]{1,0:T(8,128)(2,1)} %get-tuple-element.11), channel_id=1, source_target_pairs={{2,0},{3,1},{5,3},{7,5},{10,8},{11,9},{13,11},{15,13},{18,16},{19,... | collective-permute-start | bytes 3145736 | tf_op jit(solution)/shard_map/ppermute | solution.py:197
  46.8 54.7 %collective-permute-start.5 = (bf16[2048,256]{1,0:T(8,128)(2,1)}, bf16[2048,256]{1,0:T(8,128)(2,1)S(1)}, u32[]{:S(2)}, u32[]{:S(2)}) collective-permute-start(bf16[2048,256]{1,0:T(8,128)(2,1)} %get-tuple-element.12), channel_id=1, source_target_pairs={{5,1},{13,9},{21,17},{29,25}} | collective-permute-start | bytes 3145736 | tf_op jit(solution)/shard_map/ppermute | solution.py:197
  47.6 60.7 %collective-permute-start.7 = (bf16[2048,256]{1,0:T(8,128)(2,1)S(1)}, bf16[2048,256]{1,0:T(8,128)(2,1)}, u32[]{:S(2)}, u32[]{:S(2)}) collective-permute-start(bf16[2048,256]{1,0:T(8,128)(2,1)S(1)} %copy-done.1), channel_id=1, source_target_pairs={{0,2},{1,3},{3,5},{5,7},{8,10},{9,11},{11,13},{13,15},{16,18},{17,... | collective-permute-start | bytes 3145736 | tf_op jit(solution)/shard_map/ppermute | solution.py:197
  81.0 27.3 %collective-permute-start.8 = (bf16[2048,256]{1,0:T(8,128)(2,1)S(1)}, bf16[2048,256]{1,0:T(8,128)(2,1)}, u32[]{:S(2)}, u32[]{:S(2)}) collective-permute-start(bf16[2048,256]{1,0:T(8,128)(2,1)S(1)} %copy-done.1), channel_id=1, source_target_pairs={{1,5},{9,13},{17,21},{25,29}} | collective-permute-start | bytes 3145736 | tf_op jit(solution)/shard_map/ppermute | solution.py:197
  101.5 1.0 copy-start.5
  101.5 1.3 copy-start.6
  108.2 38.1 %collective-permute-start.6 = (bf16[1024,256]{1,0:T(8,128)(2,1)S(1)}, bf16[1024,256]{1,0:T(8,128)(2,1)S(1)}, u32[]{:S(2)}, u32[]{:S(2)}) collective-permute-start(bf16[1024,256]{1,0:T(8,128)(2,1)S(1)} %get-tuple-element.15), channel_id=1, source_target_pairs={{0,1},{1,0},{2,3},{3,2},{4,5},{5,4},{6,7},{7,6},{8,9},{9,8},{10,11... | collective-permute-start | bytes 1572872 | tf_op jit(solution)/shard_map/ppermute | solution.py:230

commit v2 on v1

v2 whole, which is shorter than its diff:
```python
import jax
import jax.numpy as jnp
from jax import lax
from jax.experimental import pallas as pl
from jax.experimental.pallas import tpu as pltpu
from jax.sharding import PartitionSpec as P


TILE = 256


def low_bit(value):
    return value & -value


def reach(chip, core, chips):
    span = low_bit(chip + 1) if core == 0 else low_bit(chip)
    return span if span < chips else 0


def place(chips):
    index = lax.axis_index("seq")
    chip, core = index // 2, index % 2
    span = jnp.where(core == 0, low_bit(chip + 1), low_bit(chip))
    return core, jnp.where(span < chips, span, 0)


def levels_of(most):
    level = 1
    while level <= most:
        yield level
        level *= 2


def dot(left, right):
    return jnp.dot(left, right, preferred_element_type=jnp.float32)


def dot_nt(left, right):
    return lax.dot_general(left, right, (((1,), (1,)), ((), ())), preferred_element_type=jnp.float32)


def ordered(side, mine, other):
    return [mine, other] if side == 0 else [other, mine]


def paired(side, refs):
    return [ordered(side, refs[at], refs[at + 1]) for at in range(0, len(refs), 2)]


def wide(stair_ref, at, pieces):
    tokens = pieces[0].shape[0]
    total = 0.0
    for index, piece in enumerate(pieces):
        total += dot(stair_ref[:, pl.ds(at + index * tokens, tokens)], piece[...])
    return total


def row_block(pieces, block):
    tokens = pieces[0].shape[0]
    start = block * TILE
    return pieces[start // tokens], start % tokens


def local_kernel(chips, filter_ref, *refs):
    grad_refs, input_refs = refs[0:2], refs[2:4]
    stair_ref, out_ref, lag_ref, early_same_ref, early_other_ref, skew_ref = refs[4:]
    tokens = grad_refs[0].shape[0]
    slab = 2 * tokens
    blocks = slab // TILE
    length = stair_ref.shape[1]
    width = skew_ref.shape[1]
    core, span = place(chips)
    row = jnp.broadcast_to(filter_ref[...], (8, width))
    skew_ref[...] = pltpu.roll(row, 0, 1, stride=1, stride_axis=0)

    def rows(step, carry):
        low = skew_ref[...]
        high = pltpu.roll(low, 8, 1)
        both = jnp.concatenate([low[:, :length], high[:, :length]], axis=0)
        stair_ref[pl.ds(pl.multiple_of(step * 16, 16), 16), :] = both.astype(stair_ref.dtype)
        skew_ref[...] = pltpu.roll(high, 8, 1)
        return carry

    lax.fori_loop(0, TILE // 16, rows, 0)
    lag_ref[...] = jnp.zeros_like(lag_ref)
    for side in range(2):

        @pl.when(core == side)
        def _(side=side):
            grads = ordered(side, *grad_refs)
            values = ordered(side, *input_refs)
            for block in range(blocks):
                start = block * TILE
                value_ref, row = row_block(values, block)
                left = value_ref[row : row + TILE, :]
                total = 0.0
                for index, piece in enumerate(grads):
                    skip = max(start - index * tokens, 0)
                    if skip >= tokens:
                        continue
                    at = index * tokens + skip - start
                    span_len = tokens - skip
                    right = piece[skip:, :]
                    total += dot(stair_ref[:, at : at + span_len], right)
                    lag_ref[:, at : at + span_len] += dot_nt(left, right)
                out_ref[start : start + TILE, :] = total

    @pl.when((core == 1) & (span == 1))
    def _():
        grads = ordered(1, *grad_refs)
        targets = ordered(1, early_same_ref, early_other_ref)
        for block in range(blocks):
            target, row = row_block(targets, block)
            part = wide(stair_ref, (blocks - block) * TILE, grads)
            target[row : row + TILE, :] = part.astype(target.dtype)


def grads_of(side, own, received):
    return received if side == 0 else [own, *received[:-1]]


def inputs_of(side, own, received):
    return [own, *received[:-1]] if side == 0 else received


def partial_rows(stair_ref, grads, low, blocks, step):
    lag = low * blocks + blocks - step
    total = 0.0
    for high, pieces in enumerate(grads):
        at = pl.multiple_of((lag + high * blocks) * TILE, TILE)
        total += wide(stair_ref, at, pieces)
    return total


def cross_kernel(chips, first, stair_ref, *refs):
    most = chips // 2
    own, received = refs[0:2], refs[2 : 2 + 2 * most]
    tokens = own[0].shape[0]
    blocks = 2 * tokens // TILE
    per = tokens // TILE
    core, span = place(chips)
    if first:
        sent = refs[2 + 2 * most :]
    else:
        local_ref = refs[2 + 2 * most]
        keep_ref, give_ref = refs[3 + 2 * most : 5 + 2 * most]
        sent = refs[5 + 2 * most :]

    for side in range(2):
        grads = grads_of(side, ordered(side, *own), paired(side, received))
        targets = paired(side, sent)
        mine = [keep_ref, give_ref] if not first else None

        def put(pieces, low, level, local=False, grads=grads, side=side):
            for index, piece in enumerate(pieces):

                def block(step, carry, index=index, piece=piece):
                    step = step + index * per
                    if level:
                        total = partial_rows(stair_ref, grads[:level], low, blocks, step)
                    else:
                        total = 0.0
                    if local:
                        total += local_ref[pl.ds(pl.multiple_of(step * TILE, TILE), TILE), :]
                    rows = pl.ds(pl.multiple_of((step - index * per) * TILE, TILE), TILE)
                    piece[rows, :] = total.astype(piece.dtype)
                    return carry

                lax.fori_loop(0, per, block, 0)

        for level in levels_of(most):

            @pl.when((core == side) & (span == level))
            def _(level=level, put=put, targets=targets, mine=mine, side=side):
                if level > 1:
                    if first:
                        put(targets[0], 1 if side == 0 else 0, level)
                    else:
                        for index, pieces in enumerate(targets):
                            low = index + (2 if side == 0 else 1)
                            if low < level:
                                put(pieces, low, level)
                if not first and side == 0:
                    put(ordered(side, *mine), 0, level, True)

        if not first:

            @pl.when((core == side) & ((side == 1) | (span == 0)))
            def _(put=put, mine=mine, side=side):
                put(ordered(side, *mine), 0, 0, True)


def lag_kernel(chips, local_ref, *refs):
    most = chips // 2
    own_grads, own_inputs = refs[0:2], refs[2:4]
    got_grads, got_inputs = refs[4 : 4 + 2 * most], refs[4 + 2 * most : 4 + 4 * most]
    out_ref, lag_ref, skew_ref = refs[4 + 4 * most :]
    tokens = own_grads[0].shape[0]
    slab = 2 * tokens
    blocks = slab // TILE
    per = tokens // TILE
    length = lag_ref.shape[1]
    core, span = place(chips)
    lag_ref[:, :slab] = local_ref[...]
    lag_ref[:, slab:] = jnp.zeros((TILE, length - slab), jnp.float32)
    for side in range(2):
        grads = grads_of(side, ordered(side, *own_grads), paired(side, got_grads))
        values = inputs_of(side, ordered(side, *own_inputs), paired(side, got_inputs))
        for level in levels_of(most):

            @pl.when((core == side) & (span == level))
            def _(grads=grads, values=values, level=level):
                for low in range(level):
                    for index, piece in enumerate(values[low]):

                        def block(step, carry, low=low, index=index, piece=piece):
                            rows = pl.ds(pl.multiple_of(step * TILE, TILE), TILE)
                            left = piece[rows, :]
                            lag = low * blocks + blocks - step - index * per
                            for high in range(level):
                                for part, right in enumerate(grads[high]):
                                    at = (lag + high * blocks + part * per) * TILE
                                    at = pl.multiple_of(at, TILE)
                                    lag_ref[:, pl.ds(at, tokens)] += dot_nt(left, right[...])
                            return carry

                        lax.fori_loop(0, per, block, 0)

    width = skew_ref.shape[1]
    skew_ref[...] = jnp.zeros_like(skew_ref)

    def rows(step, carry):
        group = TILE // 8 - 1 - step
        moved = pltpu.roll(skew_ref[...], width - 8, 1)
        part = lag_ref[pl.ds(pl.multiple_of(group * 8, 8), 8), :]
        skew_ref[...] = moved + jnp.concatenate([part, jnp.zeros((8, width - length), jnp.float32)], axis=1)
        return carry

    lax.fori_loop(0, TILE // 8, rows, 0)
    total = skew_ref[0:1, :]
    for row in range(1, 8):
        total += pltpu.roll(skew_ref[row : row + 1, :], width - row, 1)
    out_ref[...] = total[:, :length]


def finish_kernel(chips, keep_ref, given_ref, *refs):
    core, _ = place(chips)
    out_ref = refs[-1]
    half = keep_ref.shape[1]

    def total(first, parts):
        result = first[...].astype(jnp.float32)
        for part in parts:
            result += part[...].astype(jnp.float32)
        return result.astype(out_ref.dtype)

    for side in range(2):

        @pl.when(core == side)
        def _(side=side):
            mine, other = side * half, (1 - side) * half
            out_ref[:, mine : mine + half] = total(keep_ref, refs[0:-1:2])
            out_ref[:, other : other + half] = total(given_ref, refs[1:-1:2])


def call(kernel, outs, flops, scratch=()):
    return pl.pallas_call(
        kernel,
        out_shape=outs,
        scratch_shapes=scratch,
        cost_estimate=pl.CostEstimate(flops=flops, transcendentals=0, bytes_accessed=0),
    )


def on_device(inputs, grad_out, conv_filter):
    shards = lax.axis_size("seq")
    chips = shards // 2
    most = chips // 2
    core = lax.axis_index("seq") % 2
    tokens, channels = inputs.shape[1], inputs.shape[2]
    half = channels // 2
    slab = 2 * tokens
    length = shards * tokens

    def halves(array):
        return [
            lax.dynamic_slice_in_dim(array[0], start * half, half, 1) for start in (core, 1 - core)
        ]

    def swap(array):
        return lax.ppermute(array, "seq", [(index, index ^ 1) for index in range(shards)])

    def shift(pieces, distance, limit, down):
        results = []
        for turn, piece in enumerate(pieces):
            pairs = []
            for chip in range(chips):
                for side in range(2):
                    if distance > limit(reach(chip, side, chips), side):
                        continue
                    pivot = 2 * chip + side
                    if down == "out":
                        pairs.append((pivot, 2 * (chip - distance) + (side ^ turn)))
                    else:
                        away = chip + distance if down == "grad" else chip - distance
                        pairs.append((2 * away + (side ^ turn), pivot))
            results.append(lax.ppermute(piece, "seq", pairs) if pairs else jnp.zeros_like(piece))
        return results

    grad_limit = lambda span, side: span - side
    rest_limit = lambda span, side: span - 1 + side
    deep_limit = lambda span, side: rest_limit(span, side) if span > 1 else 0
    early_limit = lambda span, side: 1 if span == 1 and side == 1 else 0

    grad_mine, grad_give = halves(grad_out)
    got_grads = {}
    for distance in range(most, 0, -1):
        got_grads[distance] = shift((grad_mine, grad_give), distance, grad_limit, "grad")
    got_grads = [piece for distance in range(1, most + 1) for piece in got_grads[distance]]
    copies = jnp.broadcast_to(conv_filter[None, None], (shards, 1, tokens))
    whole_filter = lax.all_to_all(copies, "seq", 0, 1, tiled=True)
    grads = [grad_mine, swap(grad_give)]
    value_mine, value_give = halves(inputs)
    values = [value_mine, swap(value_give)]
    got_values = []
    for distance in range(1, most + 1):
        got_values += shift((value_mine, value_give), distance, rest_limit, "value")
    row = jnp.pad(whole_filter.astype(jnp.float32).reshape(1, length), ((0, 0), (0, TILE)))
    piece = jax.ShapeDtypeStruct((tokens, half), jnp.bfloat16)
    work = 2 * slab * slab * half
    stair, local_out, local_lag, early_same, early_other = call(
        lambda *refs: local_kernel(chips, *refs),
        (
            jax.ShapeDtypeStruct((TILE, length), jnp.bfloat16),
            jax.ShapeDtypeStruct((slab, half), jnp.float32),
            jax.ShapeDtypeStruct((TILE, slab), jnp.float32),
            piece,
            piece,
        ),
        2 * work,
        (pltpu.VMEM((8, length + TILE), jnp.float32),),
    )(row, *grads, *values)
    parts = shift((early_same, early_other), 1, early_limit, "out")
    sent = call(lambda *refs: cross_kernel(chips, True, *refs), (piece, piece), most * work)(stair, *grads, *got_grads)
    parts += shift(sent, 1, deep_limit, "out")
    keep, give, *sent = call(
        lambda *refs: cross_kernel(chips, False, *refs),
        (jax.ShapeDtypeStruct((tokens, half), jnp.float32), piece, *([piece] * (2 * most - 2))),
        most * work,
    )(stair, *grads, *got_grads, local_out)
    for distance in range(2, most + 1):
        parts += shift(sent[2 * distance - 4 : 2 * distance - 2], distance, deep_limit, "out")
    given = swap(give)
    filter_part = call(
        lambda *refs: lag_kernel(chips, *refs),
        jax.ShapeDtypeStruct((1, length), jnp.float32),
        most * most * work,
        (pltpu.VMEM((TILE, length), jnp.float32), pltpu.VMEM((8, length + TILE), jnp.float32)),
    )(local_lag, *grads, *values, *got_grads, *got_values)
    copies = jnp.broadcast_to(
        filter_part.reshape(1, shards, 1, tokens), (lax.axis_size("dp"), shards, 1, tokens)
    ).reshape(-1, 1, tokens)
    spread = lax.all_to_all(copies, ("dp", "seq"), 0, 1, tiled=True)
    grad_filter = jnp.sum(spread[0], axis=0)
    grad_input = call(
        lambda *refs: finish_kernel(chips, *refs),
        jax.ShapeDtypeStruct((tokens, channels), jnp.bfloat16),
        slab * channels,
    )(keep, given, *parts)
    return grad_input[None], grad_filter


def solution(mesh):
    placed = (P("dp", "seq", None), P("dp", "seq", None), P("seq"))

    return jax.shard_map(
        on_device,
        mesh=mesh,
        in_specs=placed,
        out_specs=(P("dp", "seq", None), P("seq")),
        check_vma=False,
    )
```

time: 148 us -> 122 us (0.82)
  waiting for transfers between devices: 19.7 us -> 1.49 us
  starting transfers between devices: 39.9 us -> 32.7 us
  Pallas kernels: 37.2 us -> 42.6 us
  blocking collectives: 38.3 us -> 35.3 us
  other arithmetic: 5.24 us -> 3.55 us
    all_gather x2 -> x0, blocking collectives: 22.7 us -> none  [the longest x1 14.5 us: on_device(): whole_filter = lax.all_gather(conv_filter, 'seq', tiled=True)]
    all_to_all x1, blocking collectives: 15.6 us -> 35.3 us  [on_device(): spread = lax.all_to_all(copies, ('dp', 'seq'), 0, 1, tiled=True)]
    ppermute x9 -> x17, waiting for transfers between devices: 19.7 us -> 0.04 us  [the longest x14 0.04 us: shift(): lax.ppermute(piece, 'seq', pairs)]
    ppermute x9 -> x17, starting transfers between devices: 39.9 us -> 26.8 us  [the longest x14 25.6 us: shift(): lax.ppermute(piece, 'seq', pairs)]
    all_to_all x0 -> x1, starting transfers between devices: none -> 5.98 us  [on_device(): whole_filter = lax.all_to_all(copies, 'seq', 0, 1, tiled=True)]
    pallas_call x3 -> x4, Pallas kernels: 23.6 us -> 29.2 us  [the longest x1 12.5 us: on_device(): call(lambda *refs: local_kernel(chips, *refs), (jax.ShapeDtypeStruct((TIL...]
    select_n x3 -> x0, other arithmetic: 3.96 us -> none  [the longest x2 2.75 us: to_slab(): jnp.where(core == 0, jnp.concatenate([mine, other], 0), jnp.concatenate([...]
  transfers between devices with their start and end apart: 9 -> 18, of which waited for: 2 -> 1; matrix products, arithmetic and copies ran while one was open for 4% -> 4% of each run, Pallas kernels for 19% -> 32%
where the time goes in v2:
time: 122 us
  Pallas kernels  42.6 us (35%)
  blocking collectives  35.3 us (29%)
  starting transfers between devices  32.7 us (27%)
  local copies, waits for them, and re-layouts  5.32 us (4%)
  other arithmetic  3.55 us (3%)
  waiting for transfers between devices  1.49 us (1%)
    all_to_all x1, blocking collectives, on_device(): spread = lax.all_to_all(copies, ('dp', 'seq'), 0, 1, tiled=True)  35.3 us
    ppermute x14, starting transfers between devices, shift(): lax.ppermute(piece, 'seq', pairs)  25.6 us
    pallas_call x1, Pallas kernels, on_device(): call(lambda *refs: lag_kernel(chips, *refs), jax.ShapeDtypeStruct((1, len...  13.4 us
    pallas_call x1, Pallas kernels, on_device(): call(lambda *refs: local_kernel(chips, *refs), (jax.ShapeDtypeStruct((TIL...  12.5 us
    pallas_call x1, Pallas kernels, on_device(): call(lambda *refs: cross_kernel(chips, False, *refs), (jax.ShapeDtypeStru...  9.01 us
    all_to_all x1, starting transfers between devices, on_device(): whole_filter = lax.all_to_all(copies, 'seq', 0, 1, tiled=True)  5.98 us
    pallas_call x1, Pallas kernels, on_device(): call(lambda *refs: cross_kernel(chips, True, *refs), (piece, piece), most...  4.03 us
    pallas_call x1, Pallas kernels, on_device(): call(lambda *refs: finish_kernel(chips, *refs), jax.ShapeDtypeStruct((tok...  3.75 us
  transfers between devices with their start and end apart: 18, of which 1 were waited for; matrix products, arithmetic and copies ran while one was open for 4% of the time, Pallas kernels for 32%

profile of v2, /device:TPU:0, one launch (start us, length us, event | category | flops | bytes accessed | tf_op | source)
XLA Modules:
  0.0 121.9 jit_solution(200344235046035813)
XLA Ops:
  0.6 0.0 copy-start.8
  0.6 0.0 copy-start
  0.7 2.2 %dynamic-slice_bitcast_fusion = (bf16[1024,256]{1,0:T(8,128)(2,1)S(1)}, bf16[1024,256]{1,0:T(8,128)(2,1)}) fusion(bf16[1,1024,512]{2,1,0:T(8,128)(2,1)} %param.3, s32[]{:T(128)S(6)} %select_n.17, s32[]{:T(128)S(6)} %select_n.16), kind=kLoop, calls=%fused_computation | loop fusion | bytes 2097160 | tf_op jit(solution)/shard_map/dynamic_slice | solution.py:288
  2.8 0.5 collective-permute-start.1
  3.3 0.0 copy-done.8
  3.4 0.5 broadcast.12
  3.9 0.7 reduce.6
  4.6 0.6 reshape.50
  5.2 6.0 %all-to-all-start = ((bf16[8,2,512]{2,1,0:T(2,128)(2,1)}), bf16[8,2,512]{2,1,0:T(2,128)(2,1)S(1)}, u32[]{:S(2)}, u32[]{:S(2)}) async-start(bf16[8,2,512]{2,1,0:T(2,128)(2,1)} %reshape.50), calls=%async_computation | async-start | bytes 32768 | tf_op jit(solution)/shard_map/all_to_all | solution.py:322
  11.2 0.0 copy-done
  11.2 0.1 dynamic-slice_bitcast_fusion.2
  11.3 0.0 copy-start.2
  11.3 0.7 collective-permute-start.5
  12.0 1.3 %collective-permute-start.3 = (bf16[1024,256]{1,0:T(8,128)(2,1)S(1)}, bf16[1024,256]{1,0:T(8,128)(2,1)}, u32[]{:S(2)}, u32[]{:S(2)}) collective-permute-start(bf16[1024,256]{1,0:T(8,128)(2,1)S(1)} %get-tuple-element.26), channel_id=1, source_target_pairs={{3,0},{5,2},{7,4},{6,5},{11,8},{13,10},{15,12},{14,13},{19,16},{21... | collective-permute-start | bytes 1572872 | tf_op jit(solution)/shard_map/ppermute | solution.py:308
  13.3 0.7 collective-permute-start
  14.0 1.5 %collective-permute-start.4 = (bf16[1024,256]{1,0:T(8,128)(2,1)S(1)}, bf16[1024,256]{1,0:T(8,128)(2,1)}, u32[]{:S(2)}, u32[]{:S(2)}) collective-permute-start(bf16[1024,256]{1,0:T(8,128)(2,1)S(1)} %get-tuple-element.27.refs_1_), channel_id=1, source_target_pairs={{6,2},{14,10},{22,18},{30,26}} | collective-permute-start | bytes 1572872 | tf_op jit(solution)/shard_map/ppermute | solution.py:308
  15.4 1.4 %all-to-all-done = bf16[8,2,512]{2,1,0:T(2,128)(2,1)S(1)} async-done(((bf16[8,2,512]{2,1,0:T(2,128)(2,1)}), bf16[8,2,512]{2,1,0:T(2,128)(2,1)S(1)}, u32[]{:S(2)}, u32[]{:S(2)}) %all-to-all-start) | async-done | bytes 16416 | tf_op jit(solution)/shard_map/all_to_all | solution.py:322
  16.9 0.0 collective-permute-done.1.refs_4_
  16.9 0.0 copy-start.9
  16.9 1.3 %collective-permute-start.2 = (bf16[1024,256]{1,0:T(8,128)(2,1)S(1)}, bf16[1024,256]{1,0:T(8,128)(2,1)}, u32[]{:S(2)}, u32[]{:S(2)}) collective-permute-start(bf16[1024,256]{1,0:T(8,128)(2,1)S(1)} %get-tuple-element.27.refs_1_), channel_id=1, source_target_pairs={{2,0},{4,2},{6,4},{7,5},{10,8},{12,10},{14,12},{15,13},{18,16},{20... | collective-permute-start | bytes 1572872 | tf_op jit(solution)/shard_map/ppermute | solution.py:308
  18.2 0.6 pad_convert_fusion.refs_0_
  18.8 0.0 collective-permute-done.refs_2_
  18.9 5.1 %collective-permute-start.16 = (bf16[1024,256]{1,0:T(8,128)(2,1)S(1)}, bf16[1024,256]{1,0:T(8,128)(2,1)}, u32[]{:S(2)}, u32[]{:S(2)}) collective-permute-start(bf16[1024,256]{1,0:T(8,128)(2,1)S(1)} %get-tuple-element.24), channel_id=1, source_target_pairs={{0,5},{8,13},{16,21},{24,29}} | collective-permute-start | bytes 1572872 | tf_op jit(solution)/shard_map/ppermute | solution.py:308
  24.0 0.0 copy-done.2
  24.0 0.0 copy-done.9
  24.0 12.5 %shard_map.50 = (bf16[256,8192]{1,0:T(8,128)(2,1)}, f32[2048,256]{1,0:T(8,128)}, f32[256,2048]{1,0:T(8,128)}, bf16[1024,256]{1,0:T(8,128)(2,1)}, bf16[1024,256]{1,0:T(8,128)(2,1)}) custom-call(f32[1,8448]{1,0:T(1,128)} %pad_convert_fusion.refs_0_, bf16[1024,256]{1,0:T(8,128)(2,1)} %copy-done.2, bf16[1024,256]{1,0:T(8,128)(2,1)} %collective-permute-done.refs_2_, ...), custom_call_target="tpu_custom_call" | custom-call | flops 4294967296 | tf_op jit(solution)/shard_map/pallas_call | solution.py:332
  36.4 0.0 collective-permute-done.5.refs_6_.refs_8_
  36.4 2.7 %collective-permute-start.14 = (bf16[1024,256]{1,0:T(8,128)(2,1)S(1)}, bf16[1024,256]{1,0:T(8,128)(2,1)}, u32[]{:S(2)}, u32[]{:S(2)}) collective-permute-start(bf16[1024,256]{1,0:T(8,128)(2,1)S(1)} %get-tuple-element.24), channel_id=1, source_target_pairs={{1,2},{0,3},{2,5},{4,7},{9,10},{8,11},{10,13},{12,15},{17,18},{16,... | collective-permute-start | bytes 1572872 | tf_op jit(solution)/shard_map/ppermute | solution.py:308
  39.1 0.0 collective-permute-done.3.refs_4_.refs_6_
  39.1 1.5 %collective-permute-start.15 = (bf16[1024,256]{1,0:T(8,128)(2,1)S(1)}, bf16[1024,256]{1,0:T(8,128)(2,1)}, u32[]{:S(2)}, u32[]{:S(2)}) collective-permute-start(bf16[1024,256]{1,0:T(8,128)(2,1)S(1)} %copy-done.1), channel_id=1, source_target_pairs={{1,5},{9,13},{17,21},{25,29}} | collective-permute-start | bytes 1572872 | tf_op jit(solution)/shard_map/ppermute | solution.py:308
  40.6 0.0 collective-permute-done.4.refs_5_.refs_7_
  40.6 4.8 %collective-permute-start.13 = (bf16[1024,256]{1,0:T(8,128)(2,1)S(1)}, bf16[1024,256]{1,0:T(8,128)(2,1)}, u32[]{:S(2)}, u32[]{:S(2)}) collective-permute-start(bf16[1024,256]{1,0:T(8,128)(2,1)S(1)} %copy-done.1), channel_id=1, source_target_pairs={{0,2},{1,3},{3,5},{5,7},{8,10},{9,11},{11,13},{13,15},{16,18},{17,... | collective-permute-start | bytes 1572872 | tf_op jit(solution)/shard_map/ppermute | solution.py:308
  45.4 0.0 collective-permute-done.2.refs_3_.refs_5_
  45.4 9.0 %shard_map.51 = (f32[1024,256]{1,0:T(8,128)}, bf16[1024,256]{1,0:T(8,128)(2,1)}, bf16[1024,256]{1,0:T(8,128)(2,1)}, bf16[1024,256]{1,0:T(8,128)(2,1)}) custom-call(bf16[256,8192]{1,0:T(8,128)(2,1)} %get-tuple-element.13.refs_0_, bf16[1024,256]{1,0:T(8,128)(2,1)} %copy-done.2, bf16[1024,256]{1,0:T(8,128)(2,1)} %collective-permute-done.refs_2_, ...), custom_call_target="tpu_custom_call" | custom-call | flops 4294967296 | tf_op jit(solution)/shard_map/pallas_call | solution.py:347
  54.4 0.0 collective-permute-start.6
  54.4 0.0 collective-permute-done.16.refs_12_
  54.4 0.8 collective-permute-start.11
  55.2 4.0 %shard_map.52 = (bf16[1024,256]{1,0:T(8,128)(2,1)}, bf16[1024,256]{1,0:T(8,128)(2,1)}) custom-call(bf16[256,8192]{1,0:T(8,128)(2,1)} %get-tuple-element.13.refs_0_, bf16[1024,256]{1,0:T(8,128)(2,1)} %copy-done.2, bf16[1024,256]{1,0:T(8,128)(2,1)} %collective-permute-done.refs_2_, bf16[1024,256]{1,0:T(8,128)(2,1)} %collective-permute-done.2.refs_3_.refs_5_, ...), custom_call_target="tpu_custom_call" | custom-call | flops 4294967296 | tf_op jit(solution)/shard_map/pallas_call | solution.py:345
  59.3 0.0 collective-permute-done.14.refs_10_
  59.3 1.3 %collective-permute-start.12 = (bf16[1024,256]{1,0:T(8,128)(2,1)}, bf16[1024,256]{1,0:T(8,128)(2,1)S(1)}, u32[]{:S(2)}, u32[]{:S(2)}) collective-permute-start(bf16[1024,256]{1,0:T(8,128)(2,1)} %get-tuple-element.22), channel_id=1, source_target_pairs={{5,0},{13,8},{21,16},{29,24}} | collective-permute-start | bytes 1572872 | tf_op jit(solution)/shard_map/ppermute | solution.py:308
  60.6 0.0 collective-permute-done.15.refs_11_
  60.6 1.3 %collective-permute-start.9 = (bf16[1024,256]{1,0:T(8,128)(2,1)}, bf16[1024,256]{1,0:T(8,128)(2,1)S(1)}, u32[]{:S(2)}, u32[]{:S(2)}) collective-permute-start(bf16[1024,256]{1,0:T(8,128)(2,1)} %get-tuple-element.19), channel_id=1, source_target_pairs={{2,0},{5,3},{10,8},{13,11},{18,16},{21,19},{26,24},{29,27}} | collective-permute-start | bytes 1572872 | tf_op jit(solution)/shard_map/ppermute | solution.py:308
  61.9 0.0 collective-permute-done.13.refs_9_
  61.9 0.7 collective-permute-start.10
  62.6 0.0 collective-permute-done.6.refs_1_
  62.6 0.0 copy-start.3
  62.6 1.5 %collective-permute-start.7 = (bf16[1024,256]{1,0:T(8,128)(2,1)}, bf16[1024,256]{1,0:T(8,128)(2,1)}, u32[]{:S(2)}, u32[]{:S(2)}) collective-permute-start(bf16[1024,256]{1,0:T(8,128)(2,1)} %get-tuple-element.17), channel_id=1, source_target_pairs={{3,1},{7,5},{11,9},{15,13},{19,17},{23,21},{27,25},{31,29}} | collective-permute-start | bytes 1572872 | tf_op jit(solution)/shard_map/ppermute | solution.py:308
  64.1 0.0 collective-permute-done.11.refs_6_
  64.1 1.3 %collective-permute-start.8 = (bf16[1024,256]{1,0:T(8,128)(2,1)S(1)}, bf16[1024,256]{1,0:T(8,128)(2,1)}, u32[]{:S(2)}, u32[]{:S(2)}) collective-permute-start(bf16[1024,256]{1,0:T(8,128)(2,1)S(1)} %copy-done.11), channel_id=1, source_target_pairs={{3,0},{7,4},{11,8},{15,12},{19,16},{23,20},{27,24},{31,28}} | collective-permute-start | bytes 1572872 | tf_op jit(solution)/shard_map/ppermute | solution.py:308
  65.4 13.4 %shard_map.54 = f32[1,8192]{1,0:T(1,128)} custom-call(f32[256,2048]{1,0:T(8,128)} %get-tuple-element.23.refs_0_, bf16[1024,256]{1,0:T(8,128)(2,1)} %copy-done.2, bf16[1024,256]{1,0:T(8,128)(2,1)} %collective-permute-done.refs_2_, bf16[1024,256]{1,0:T(8,128)(2,1)} %get-tuple-element.25.refs_3_, bf16[1024,256]{1,0:T(8,128)(2,1)} %copy-done.9, ...), custom_call_target="tpu_custom_call" | custom-call | flops 8589934592 | tf_op jit(solution)/shard_map/pallas_call | solution.py:355
  78.8 0.5 broadcast.11
  79.3 1.5 %reduce.5 = f32[8192]{0:T(1024)S(1)} reduce(f32[1,8192]{1,0:T(1,128)} %shard_map.54, f32[]{:T(128)} %broadcast.11), dimensions={0}, to_apply=%pallas_call.41.reduce_sub_computation.3 | reduce | bytes 65540 | tf_op jit(solution)/shard_map/pallas_call | solution.py:355
  80.8 0.2 broadcast_in_dim.22
  80.9 35.3 %all_to_all.8 = f32[32,1,1024]{2,1,0:T(1,128)S(1)} all-to-all(f32[32,1,1024]{2,1,0:T(1,128)S(1)} %broadcast_in_dim.22), channel_id=1, replica_groups=mesh['dp'=4,'seq'=8] {'dp','seq'}, dimensions={0} | all-to-all | bytes 262144 | tf_op jit(solution)/shard_map/all_to_all | solution.py:364
  116.2 0.7 reduce_sum.9
  116.9 0.0 collective-permute-done.12.refs_7_
  116.9 0.0 collective-permute-done.9.refs_4_
  116.9 0.0 collective-permute-done.10.refs_5_
  116.9 0.0 collective-permute-done.7.refs_2_
  116.9 0.0 collective-permute-done.8.refs_3_
  116.9 0.8 copy-done.5
  117.7 0.2 copy-done.6
  117.9 0.2 copy-done.7
  118.1 3.8 %shard_map.53 = bf16[1024,512]{1,0:T(8,128)(2,1)} custom-call(f32[1024,256]{1,0:T(8,128)} %get-tuple-element.15.refs_0_, bf16[1024,256]{1,0:T(8,128)(2,1)} %copy-done.3, bf16[1024,256]{1,0:T(8,128)(2,1)} %collective-permute-done.7.refs_2_, bf16[1024,256]{1,0:T(8,128)(2,1)} %collective-permute-done.8.refs_3_, bf16[1024,256]{1,0:T(8,128)(2,1)} %copy-done.6, ...), custom_call_target="tpu_custom_call" | custom-call | flops 1048576 | tf_op jit(solution)/shard_map/pallas_call | solution.py:366
  (16 shorter events, 0.1 us)
Async XLA Ops:
  0.6 2.7 %copy-start.8 = (bf16[1024]{0:T(1024)(128)(2,1)S(1)}, bf16[1024]{0:T(1024)(128)(2,1)}, u32[]{:S(2)}) copy-start(bf16[1024]{0:T(1024)(128)(2,1)} %param.5) | copy-start | bytes 6148
  0.6 10.6 %copy-start = (bf16[1,1024,512]{2,1,0:T(8,128)(2,1)S(1)}, bf16[1,1024,512]{2,1,0:T(8,128)(2,1)}, u32[]{:S(2)}) copy-start(bf16[1,1024,512]{2,1,0:T(8,128)(2,1)} %param.4) | copy-start | bytes 3145732
  2.8 14.0 %collective-permute-start.1 = (bf16[1024,256]{1,0:T(8,128)(2,1)S(1)}, bf16[1024,256]{1,0:T(8,128)(2,1)S(1)}, u32[]{:S(2)}, u32[]{:S(2)}) collective-permute-start(bf16[1024,256]{1,0:T(8,128)(2,1)S(1)} %get-tuple-element.24), channel_id=1, source_target_pairs={{0,1},{1,0},{2,3},{3,2},{4,5},{5,4},{6,7},{7,6},{8,9},{9,8},{10,11... | collective-permute-start | bytes 1572872 | tf_op jit(solution)/shard_map/ppermute | solution.py:292
  5.2 11.6 %all-to-all-start = ((bf16[8,2,512]{2,1,0:T(2,128)(2,1)}), bf16[8,2,512]{2,1,0:T(2,128)(2,1)S(1)}, u32[]{:S(2)}, u32[]{:S(2)}) async-start(bf16[8,2,512]{2,1,0:T(2,128)(2,1)} %reshape.50), calls=%async_computation | async-start | bytes 32768 | tf_op jit(solution)/shard_map/all_to_all | solution.py:322
  11.3 12.7 %copy-start.2 = (bf16[1024,256]{1,0:T(8,128)(2,1)}, bf16[1024,256]{1,0:T(8,128)(2,1)S(1)}, u32[]{:S(2)}) copy-start(bf16[1024,256]{1,0:T(8,128)(2,1)S(1)} %get-tuple-element.27.refs_1_) | copy-start | bytes 1572868
  11.3 25.1 %collective-permute-start.5 = (bf16[1024,256]{1,0:T(8,128)(2,1)S(1)}, bf16[1024,256]{1,0:T(8,128)(2,1)S(1)}, u32[]{:S(2)}, u32[]{:S(2)}) collective-permute-start(bf16[1024,256]{1,0:T(8,128)(2,1)S(1)} %get-tuple-element.26), channel_id=1, source_target_pairs={{7,2},{15,10},{23,18},{31,26}} | collective-permute-start | bytes 1572872 | tf_op jit(solution)/shard_map/ppermute | solution.py:308
  12.0 27.1 %collective-permute-start.3 = (bf16[1024,256]{1,0:T(8,128)(2,1)S(1)}, bf16[1024,256]{1,0:T(8,128)(2,1)}, u32[]{:S(2)}, u32[]{:S(2)}) collective-permute-start(bf16[1024,256]{1,0:T(8,128)(2,1)S(1)} %get-tuple-element.26), channel_id=1, source_target_pairs={{3,0},{5,2},{7,4},{6,5},{11,8},{13,10},{15,12},{14,13},{19,16},{21... | collective-permute-start | bytes 1572872 | tf_op jit(solution)/shard_map/ppermute | solution.py:308
  13.3 5.5 %collective-permute-start = (bf16[1024,256]{1,0:T(8,128)(2,1)S(1)}, bf16[1024,256]{1,0:T(8,128)(2,1)}, u32[]{:S(2)}, u32[]{:S(2)}) collective-permute-start(bf16[1024,256]{1,0:T(8,128)(2,1)S(1)} %get-tuple-element.26), channel_id=1, source_target_pairs={{0,1},{1,0},{2,3},{3,2},{4,5},{5,4},{6,7},{7,6},{8,9},{9,8},{10,11... | collective-permute-start | bytes 1572872 | tf_op jit(solution)/shard_map/ppermute | solution.py:292
  14.0 26.6 %collective-permute-start.4 = (bf16[1024,256]{1,0:T(8,128)(2,1)S(1)}, bf16[1024,256]{1,0:T(8,128)(2,1)}, u32[]{:S(2)}, u32[]{:S(2)}) collective-permute-start(bf16[1024,256]{1,0:T(8,128)(2,1)S(1)} %get-tuple-element.27.refs_1_), channel_id=1, source_target_pairs={{6,2},{14,10},{22,18},{30,26}} | collective-permute-start | bytes 1572872 | tf_op jit(solution)/shard_map/ppermute | solution.py:308
  16.9 7.1 %copy-start.9 = (bf16[1024,256]{1,0:T(8,128)(2,1)}, bf16[1024,256]{1,0:T(8,128)(2,1)S(1)}, u32[]{:S(2)}) copy-start(bf16[1024,256]{1,0:T(8,128)(2,1)S(1)} %collective-permute-done.1.refs_4_) | copy-start | bytes 1572868
  16.9 28.5 %collective-permute-start.2 = (bf16[1024,256]{1,0:T(8,128)(2,1)S(1)}, bf16[1024,256]{1,0:T(8,128)(2,1)}, u32[]{:S(2)}, u32[]{:S(2)}) collective-permute-start(bf16[1024,256]{1,0:T(8,128)(2,1)S(1)} %get-tuple-element.27.refs_1_), channel_id=1, source_target_pairs={{2,0},{4,2},{6,4},{7,5},{10,8},{12,10},{14,12},{15,13},{18,16},{20... | collective-permute-start | bytes 1572872 | tf_op jit(solution)/shard_map/ppermute | solution.py:308
  18.9 35.5 %collective-permute-start.16 = (bf16[1024,256]{1,0:T(8,128)(2,1)S(1)}, bf16[1024,256]{1,0:T(8,128)(2,1)}, u32[]{:S(2)}, u32[]{:S(2)}) collective-permute-start(bf16[1024,256]{1,0:T(8,128)(2,1)S(1)} %get-tuple-element.24), channel_id=1, source_target_pairs={{0,5},{8,13},{16,21},{24,29}} | collective-permute-start | bytes 1572872 | tf_op jit(solution)/shard_map/ppermute | solution.py:308
  24.0 15.1 %copy-start.1 = (bf16[1024,256]{1,0:T(8,128)(2,1)S(1)}, bf16[1024,256]{1,0:T(8,128)(2,1)}, u32[]{:S(2)}) copy-start(bf16[1024,256]{1,0:T(8,128)(2,1)} %get-tuple-element.25.refs_3_) | copy-start | bytes 1572868
  36.4 9.0 %copy-start.10 = (bf16[1024,256]{1,0:T(8,128)(2,1)}, bf16[1024,256]{1,0:T(8,128)(2,1)S(1)}, u32[]{:S(2)}) copy-start(bf16[1024,256]{1,0:T(8,128)(2,1)S(1)} %collective-permute-done.5.refs_6_.refs_8_) | copy-start | bytes 1572868
  36.4 22.8 %collective-permute-start.14 = (bf16[1024,256]{1,0:T(8,128)(2,1)S(1)}, bf16[1024,256]{1,0:T(8,128)(2,1)}, u32[]{:S(2)}, u32[]{:S(2)}) collective-permute-start(bf16[1024,256]{1,0:T(8,128)(2,1)S(1)} %get-tuple-element.24), channel_id=1, source_target_pairs={{1,2},{0,3},{2,5},{4,7},{9,10},{8,11},{10,13},{12,15},{17,18},{16,... | collective-permute-start | bytes 1572872 | tf_op jit(solution)/shard_map/ppermute | solution.py:308
  39.1 21.5 %collective-permute-start.15 = (bf16[1024,256]{1,0:T(8,128)(2,1)S(1)}, bf16[1024,256]{1,0:T(8,128)(2,1)}, u32[]{:S(2)}, u32[]{:S(2)}) collective-permute-start(bf16[1024,256]{1,0:T(8,128)(2,1)S(1)} %copy-done.1), channel_id=1, source_target_pairs={{1,5},{9,13},{17,21},{25,29}} | collective-permute-start | bytes 1572872 | tf_op jit(solution)/shard_map/ppermute | solution.py:308
  40.6 21.3 %collective-permute-start.13 = (bf16[1024,256]{1,0:T(8,128)(2,1)S(1)}, bf16[1024,256]{1,0:T(8,128)(2,1)}, u32[]{:S(2)}, u32[]{:S(2)}) collective-permute-start(bf16[1024,256]{1,0:T(8,128)(2,1)S(1)} %copy-done.1), channel_id=1, source_target_pairs={{0,2},{1,3},{3,5},{5,7},{8,10},{9,11},{11,13},{13,15},{16,18},{17,... | collective-permute-start | bytes 1572872 | tf_op jit(solution)/shard_map/ppermute | solution.py:308
  54.4 8.2 %collective-permute-start.6 = (bf16[1024,256]{1,0:T(8,128)(2,1)}, bf16[1024,256]{1,0:T(8,128)(2,1)S(1)}, u32[]{:S(2)}, u32[]{:S(2)}) collective-permute-start(bf16[1024,256]{1,0:T(8,128)(2,1)} %get-tuple-element.16), channel_id=1, source_target_pairs={{0,1},{1,0},{2,3},{3,2},{4,5},{5,4},{6,7},{7,6},{8,9},{9,8},{10,11... | collective-permute-start | bytes 1572872 | tf_op jit(solution)/shard_map/ppermute | solution.py:292
  54.4 9.7 %copy-start.11 = (bf16[1024,256]{1,0:T(8,128)(2,1)S(1)}, bf16[1024,256]{1,0:T(8,128)(2,1)}, u32[]{:S(2)}) copy-start(bf16[1024,256]{1,0:T(8,128)(2,1)} %get-tuple-element.18) | copy-start | bytes 1572868
  54.4 9.7 %collective-permute-start.11 = (bf16[1024,256]{1,0:T(8,128)(2,1)}, bf16[1024,256]{1,0:T(8,128)(2,1)S(1)}, u32[]{:S(2)}, u32[]{:S(2)}) collective-permute-start(bf16[1024,256]{1,0:T(8,128)(2,1)} %get-tuple-element.21), channel_id=1, source_target_pairs={{5,1},{13,9},{21,17},{29,25}} | collective-permute-start | bytes 1572872 | tf_op jit(solution)/shard_map/ppermute | solution.py:308
  59.3 57.6 %collective-permute-start.12 = (bf16[1024,256]{1,0:T(8,128)(2,1)}, bf16[1024,256]{1,0:T(8,128)(2,1)S(1)}, u32[]{:S(2)}, u32[]{:S(2)}) collective-permute-start(bf16[1024,256]{1,0:T(8,128)(2,1)} %get-tuple-element.22), channel_id=1, source_target_pairs={{5,0},{13,8},{21,16},{29,24}} | collective-permute-start | bytes 1572872 | tf_op jit(solution)/shard_map/ppermute | solution.py:308
  60.6 56.3 %collective-permute-start.9 = (bf16[1024,256]{1,0:T(8,128)(2,1)}, bf16[1024,256]{1,0:T(8,128)(2,1)S(1)}, u32[]{:S(2)}, u32[]{:S(2)}) collective-permute-start(bf16[1024,256]{1,0:T(8,128)(2,1)} %get-tuple-element.19), channel_id=1, source_target_pairs={{2,0},{5,3},{10,8},{13,11},{18,16},{21,19},{26,24},{29,27}} | collective-permute-start | bytes 1572872 | tf_op jit(solution)/shard_map/ppermute | solution.py:308
  61.9 55.0 %collective-permute-start.10 = (bf16[1024,256]{1,0:T(8,128)(2,1)}, bf16[1024,256]{1,0:T(8,128)(2,1)S(1)}, u32[]{:S(2)}, u32[]{:S(2)}) collective-permute-start(bf16[1024,256]{1,0:T(8,128)(2,1)} %get-tuple-element.20), channel_id=1, source_target_pairs={{2,1},{5,2},{10,9},{13,10},{18,17},{21,18},{26,25},{29,26}} | collective-permute-start | bytes 1572872 | tf_op jit(solution)/shard_map/ppermute | solution.py:308
  62.6 16.2 %copy-start.3 = (bf16[1024,256]{1,0:T(8,128)(2,1)}, bf16[1024,256]{1,0:T(8,128)(2,1)S(1)}, u32[]{:S(2)}) copy-start(bf16[1024,256]{1,0:T(8,128)(2,1)S(1)} %collective-permute-done.6.refs_1_) | copy-start | bytes 1572868
  62.6 54.3 %collective-permute-start.7 = (bf16[1024,256]{1,0:T(8,128)(2,1)}, bf16[1024,256]{1,0:T(8,128)(2,1)}, u32[]{:S(2)}, u32[]{:S(2)}) collective-permute-start(bf16[1024,256]{1,0:T(8,128)(2,1)} %get-tuple-element.17), channel_id=1, source_target_pairs={{3,1},{7,5},{11,9},{15,13},{19,17},{23,21},{27,25},{31,29}} | collective-permute-start | bytes 1572872 | tf_op jit(solution)/shard_map/ppermute | solution.py:308
  64.1 14.7 %copy-start.4 = (bf16[1024,256]{1,0:T(8,128)(2,1)}, bf16[1024,256]{1,0:T(8,128)(2,1)S(1)}, u32[]{:S(2)}) copy-start(bf16[1024,256]{1,0:T(8,128)(2,1)S(1)} %collective-permute-done.11.refs_6_) | copy-start | bytes 1572868
  64.1 52.9 %collective-permute-start.8 = (bf16[1024,256]{1,0:T(8,128)(2,1)S(1)}, bf16[1024,256]{1,0:T(8,128)(2,1)}, u32[]{:S(2)}, u32[]{:S(2)}) collective-permute-start(bf16[1024,256]{1,0:T(8,128)(2,1)S(1)} %copy-done.11), channel_id=1, source_target_pairs={{3,0},{7,4},{11,8},{15,12},{19,16},{23,20},{27,24},{31,28}} | collective-permute-start | bytes 1572872 | tf_op jit(solution)/shard_map/ppermute | solution.py:308
  116.9 0.8 copy-start.5
  116.9 1.0 copy-start.6
  116.9 1.2 copy-start.7
